TPU v7x, 512 devices: a 8x2x16 block of a 8x8x16 slice. The times are simulated.
512 devices in a mesh: grp: 2 (over y), sp: 16 (over z), blk: 8 (over x), rep: 2 (over core).
Axes of the slice: x: 8, y: 2, z: 16, core: 2. Of those that a mesh axis runs over, the one named last changes fastest.
The devices are a block of a 8x8x16 slice.
Arguments:
- hidden: bfloat16 [16, 2048, 4096], P(('grp', 'blk'), 'sp'), parts along dimension 0, may hold values from -64 to 64
- queries: bfloat16 [16, 2048, 4096], P(('grp', 'blk'), 'sp', 'rep'), parts along dimension 0, may hold values from -600 to 600
- norm_gain: float32 [4096], replicated, may hold values from 0.1 to 1.9
- key_matrix: bfloat16 [4096, 1024], P('sp', 'rep'), may hold values from -0.09375 to 0.09375
- value_matrix: bfloat16 [4096, 1024], P('sp', 'rep'), may hold values from -0.09375 to 0.09375
- key_shift_bias: bfloat16 [1024], P('rep'), may hold values from -3 to 3
- value_shift_bias: bfloat16 [1024], P('rep'), may hold values from -3 to 3
- doc_lengths: int32 [16], P('grp'), parts along dimension 0, may hold values from 1 to 4097, 16384 in all
Outputs:
- attended: bfloat16 [16, 2048, 4096], P(('grp', 'blk'), 'sp', 'rep'), parts along dimension 0
There are 2 independent parts, one for each index of `grp`. A program takes and returns all parts, laid end to end along the dimension named above; an argument that names none is the same for every part. Nothing has to cross between parts.
Inputs may be any that keep to these rules, and one draw needn't show every extreme that they name: `doc_lengths`: the lengths of the 8 documents packed in order into the sequence; they sum to 16384, and the longest is exactly 4097 tokens.
All inputs are finite; a program needn't handle non-finite values.
Results may differ from a plain program's by a relative error of at most 0.012.
The roundings to bfloat16 on the way count: a program that leaves them out, or rounds other values in their place, can miss the bound.
Values may be sent and summed in bfloat16 or wider, within the bound.
No kernel may reach another device: no remote copies, remote signals or barrier semaphores. Data moves between devices by JAX's collectives and lax.ppermute only.
A program may use at most 64 MiB of HBM per device.

v0:
```python
import functools
import math

import jax
import jax.numpy as jnp
from jax import lax
from jax.experimental import pallas as pl
from jax.experimental.pallas import tpu as pltpu
from jax.sharding import PartitionSpec as P

HEAD = 128
EPS_VALUE = 1e-06
THETA_BASE = 1000000.0
START_MAX = -1e30
HIDDEN_SCORE = -3e38
EXP2_SCALE = math.log2(math.e) / math.sqrt(HEAD)
PIECE = 512
TILE = 128
ROWS = 256


def apply_rotation(projected, token_places):
    half_size = projected.shape[-1] // 2
    freq_index = jnp.arange(half_size).astype(jnp.float32)
    inverse = jnp.exp(freq_index * (-2.0 * math.log(THETA_BASE) / projected.shape[-1]))
    angles = token_places[:, None] * inverse[None, :]
    cosine = jnp.cos(angles)[:, None, :]
    sine = jnp.sin(angles)[:, None, :]
    first_half = projected[..., :half_size]
    second_half = projected[..., half_size:]
    return jnp.concatenate(
        [first_half * cosine - second_half * sine, second_half * cosine + first_half * sine],
        axis=-1,
    )


def attention_kernel(blocks, heads, first, last, info, docs, q_ref, *refs):
    keys, values = refs[:blocks], refs[blocks : 2 * blocks]
    rest = list(refs[2 * blocks :])
    if not first:
        max_in, sum_in = rest[0], rest[1]
        rest = rest[2:]
    if last:
        out_ref = rest[0]
        max_ref, sum_ref = rest[1], rest[2]
        rest = rest[3:]
    else:
        max_ref, sum_ref = rest[0], rest[1]
        rest = rest[2:]
    stacked = rest[0]
    bounds = rest[1]
    tiles = q_ref.shape[0] // TILE
    count = docs.shape[0]
    pieces = keys[0].shape[0] // PIECE
    query_base = info[0]

    ends = []
    total = 0
    for d in range(count):
        total = total + docs[d]
        ends.append(total)

    def start_of(place):
        begin = 0
        for end in ends:
            begin = jnp.where(end <= place, end, begin)
        return begin

    for i in range(tiles):
        low = query_base + i * TILE
        bounds[2 * i] = start_of(low)
        bounds[2 * i + 1] = start_of(low + TILE - 1)
        for h in range(heads):
            stacked[i, h * TILE : (h + 1) * TILE, :] = q_ref[
                i * TILE : (i + 1) * TILE, h * HEAD : (h + 1) * HEAD
            ]
    if first:
        max_ref[...] = jnp.full(max_ref.shape, START_MAX, jnp.float32)
        sum_ref[...] = jnp.zeros(sum_ref.shape, jnp.float32)
    else:
        max_ref[...] = max_in[...]
        sum_ref[...] = sum_in[...]

    def step(key_ref, value_ref, piece, i, low, key_low, masked):
        key_rows = pl.ds(pl.multiple_of(piece * PIECE, PIECE), PIECE)
        key = key_ref[key_rows, :]
        value = jnp.concatenate(
            [value_ref[key_rows, :], jnp.ones((PIECE, HEAD), jnp.bfloat16)], axis=1
        )
        visible = None
        if masked:
            row_place = low + lax.broadcasted_iota(jnp.int32, (TILE, HEAD), 0)
            begin = jnp.zeros((TILE, HEAD), jnp.int32)
            for end in ends:
                begin = jnp.where(row_place >= end, end, begin)
            lanes = lax.broadcasted_iota(jnp.int32, (TILE, HEAD), 1)
            parts = []
            for part in range(PIECE // HEAD):
                key_place = lanes + (key_low + part * HEAD)
                parts.append((key_place <= row_place) & (key_place >= begin))
            visible = jnp.concatenate(parts, axis=1)
        for r in range(heads * TILE // ROWS):
            rows = slice(r * ROWS, (r + 1) * ROWS)
            scores = lax.dot_general(
                stacked[i, rows, :],
                key,
                (((1,), (1,)), ((), ())),
                preferred_element_type=jnp.float32,
            )
            if masked:
                scores = jnp.concatenate(
                    [
                        jnp.where(visible, scores[k * TILE : (k + 1) * TILE], HIDDEN_SCORE)
                        for k in range(ROWS // TILE)
                    ],
                    axis=0,
                )
            old_max = max_ref[i, rows, :]
            new_max = jnp.maximum(old_max, jnp.max(scores, axis=1, keepdims=True))
            factor = jnp.exp2((old_max - new_max) * EXP2_SCALE)
            weights = jnp.exp2(
                (scores - jnp.concatenate([new_max] * (PIECE // HEAD), axis=1)) * EXP2_SCALE
            ).astype(jnp.bfloat16)
            added = lax.dot_general(
                weights, value, (((1,), (0,)), ((), ())), preferred_element_type=jnp.float32
            )
            sum_ref[i, rows, :] = (
                sum_ref[i, rows, :] * jnp.concatenate([factor, factor], axis=1) + added
            )
            max_ref[i, rows, :] = new_max

    for j in range(blocks):
        key_base = info[1 + j]

        def over_pieces(piece, carry, j=j, key_base=key_base):
            key_low = key_base + piece * PIECE

            def over_tiles(i, inner):
                low = query_base + i * TILE
                reached = (key_low <= low + TILE - 1) & (
                    key_low + PIECE - 1 >= bounds[2 * i]
                )
                whole = (key_low + PIECE - 1 <= low) & (key_low >= bounds[2 * i + 1])

                @pl.when(reached & whole)
                def _():
                    step(keys[j], values[j], piece, i, low, key_low, False)

                @pl.when(reached & jnp.logical_not(whole))
                def _():
                    step(keys[j], values[j], piece, i, low, key_low, True)

                return inner

            return lax.fori_loop(0, tiles, over_tiles, carry)

        lax.fori_loop(0, pieces, over_pieces, 0)

    if last:
        for i in range(tiles):
            for h in range(heads):
                rows = slice(h * TILE, (h + 1) * TILE)
                out_ref[i * TILE : (i + 1) * TILE, h * HEAD : (h + 1) * HEAD] = (
                    sum_ref[i, rows, :HEAD] / sum_ref[i, rows, HEAD:]
                ).astype(jnp.bfloat16)


def attend(info, docs, query, keys, values, state, last):
    tokens = query.shape[0]
    heads = query.shape[1] // HEAD
    tiles = tokens // TILE
    blocks = len(keys)
    first = state is None
    max_shape = (tiles, heads * TILE, HEAD)
    sum_shape = (tiles, heads * TILE, 2 * HEAD)
    vmem = pl.BlockSpec(memory_space=pltpu.VMEM)
    smem = pl.BlockSpec(memory_space=pltpu.SMEM)
    held = [pltpu.VMEM(max_shape, jnp.float32), pltpu.VMEM(sum_shape, jnp.float32)]
    scratch = [
        pltpu.VMEM((tiles, heads * TILE, HEAD), jnp.bfloat16),
        pltpu.SMEM((2 * tiles,), jnp.int32),
    ]
    if last:
        out_shape = jax.ShapeDtypeStruct((tokens, heads * HEAD), jnp.bfloat16)
        out_specs = vmem
        scratch = held + scratch
    else:
        out_shape = (
            jax.ShapeDtypeStruct(max_shape, jnp.float32),
            jax.ShapeDtypeStruct(sum_shape, jnp.float32),
        )
        out_specs = (vmem, vmem)
    operands = [query, *keys, *values] + ([] if first else list(state))
    pairs = tokens * heads * keys[0].shape[0] * blocks
    return pl.pallas_call(
        functools.partial(attention_kernel, blocks, heads, first, last),
        out_shape=out_shape,
        in_specs=[smem, smem] + [vmem] * len(operands),
        out_specs=out_specs,
        scratch_shapes=scratch,
        name="attend_last" if last else "attend_first",
        cost_estimate=pl.CostEstimate(
            flops=pairs * 4 * HEAD, bytes_accessed=4 << 20, transcendentals=pairs
        ),
        compiler_params=pltpu.CompilerParams(vmem_limit_bytes=40 << 20),
    )(info, docs, *operands)


def on_device(
    hidden,
    queries,
    norm_gain,
    key_matrix,
    value_matrix,
    key_shift_bias,
    value_shift_bias,
    doc_lengths,
):
    sp_count = lax.axis_size("sp")
    blk_count = lax.axis_size("blk")
    sp_place = lax.axis_index("sp")
    blk_place = lax.axis_index("blk")
    rep_place = lax.axis_index("rep")
    local_rows = hidden.shape[1]
    width = hidden.shape[2]
    span_rows = local_rows * sp_count
    kv_local = key_matrix.shape[1] // HEAD
    quads = sp_count // kv_local
    quad_rows = local_rows * kv_local
    side = blk_place % 2
    half_heads = kv_local // 2
    half_columns = half_heads * HEAD

    near = [[q * kv_local + i for i in range(kv_local)] for q in range(quads)]
    swap = [(b, b ^ 1) for b in range(blk_count)]
    ahead = [(b, (b + 1) % blk_count) for b in range(blk_count)]
    behind = [((b + 1) % blk_count, b) for b in range(blk_count)]

    picked = jnp.concatenate(
        [
            lax.dynamic_slice_in_dim(key_matrix, side * half_columns, half_columns, 1),
            lax.dynamic_slice_in_dim(value_matrix, side * half_columns, half_columns, 1),
        ],
        axis=1,
    )
    weight = lax.all_gather(picked, "sp", axis=0, tiled=True)

    rows_all = hidden[0].astype(jnp.float32)
    row_scale = lax.rsqrt(jnp.mean(rows_all * rows_all, axis=1, keepdims=True) + EPS_VALUE)
    normed = (rows_all * row_scale * norm_gain).astype(jnp.bfloat16)
    half_width = width // 2
    mine = lax.dynamic_slice_in_dim(normed, rep_place * half_width, half_width, 1)
    theirs = lax.ppermute(mine, "blk", swap)
    theirs_other = lax.ppermute(theirs, "rep", [(0, 1), (1, 0)])
    is_low = rep_place == 0
    partner = jnp.concatenate(
        [
            jnp.where(is_low, theirs, theirs_other),
            jnp.where(is_low, theirs_other, theirs),
        ],
        axis=1,
    )
    both = jnp.concatenate([normed, partner], axis=0)

    query_moved = lax.ppermute(queries[0], "blk", behind)
    query = lax.all_to_all(
        query_moved, "sp", split_axis=1, concat_axis=0, tiled=True, axis_index_groups=near
    )

    projected = jnp.dot(both, weight, preferred_element_type=jnp.float32)
    bias = jnp.concatenate(
        [
            lax.dynamic_slice_in_dim(key_shift_bias, side * half_columns, half_columns, 0),
            lax.dynamic_slice_in_dim(value_shift_bias, side * half_columns, half_columns, 0),
        ]
    ).astype(jnp.float32)
    projected = projected + bias
    local_places = sp_place * local_rows + jnp.arange(local_rows)
    places = jnp.concatenate(
        [local_places + blk_place * span_rows, local_places + (blk_place ^ 1) * span_rows]
    )
    keys_new = apply_rotation(
        projected[:, :half_columns].reshape(2 * local_rows, half_heads, HEAD),
        places.astype(jnp.float32),
    ).astype(jnp.bfloat16)
    values_new = (
        projected[:, half_columns:]
        .reshape(2 * local_rows, half_heads, HEAD)
        .astype(jnp.bfloat16)
    )
    pair_new = jnp.concatenate([keys_new, values_new], axis=2).reshape(
        2 * local_rows, half_heads * 2 * HEAD
    )
    kept = pair_new[:local_rows]
    other = lax.ppermute(pair_new[local_rows:], "blk", swap)
    even = side == 0
    all_heads = jnp.concatenate(
        [jnp.where(even, kept, other), jnp.where(even, other, kept)], axis=1
    )
    def to_heads(part):
        one = all_heads.reshape(local_rows, kv_local, 2 * HEAD)[:, :, part * HEAD : (part + 1) * HEAD]
        sent = jnp.tile(one.reshape(local_rows, kv_local * HEAD), (1, quads))
        return lax.all_to_all(sent, "sp", split_axis=1, concat_axis=0, tiled=True)

    key_block = to_heads(0)
    value_block = to_heads(1)
    key_next = lax.ppermute(key_block, "blk", behind)
    key_prior = lax.ppermute(key_block, "blk", ahead)
    value_next = lax.ppermute(value_block, "blk", behind)
    value_prior = lax.ppermute(value_block, "blk", ahead)

    query_block = (blk_place + 1) % blk_count
    base = query_block * span_rows
    query_base = base + sp_place // kv_local * quad_rows
    info_first = jnp.stack([query_base, base - span_rows]).astype(jnp.int32)
    info_last = jnp.stack([query_base, base, base - 2 * span_rows]).astype(jnp.int32)
    state = attend(info_first, doc_lengths, query, [key_block], [value_block], None, False)
    result = attend(
        info_last,
        doc_lengths,
        query,
        [key_next, key_prior],
        [value_next, value_prior],
        state,
        True,
    )
    spread = lax.all_to_all(
        result, "sp", split_axis=0, concat_axis=1, tiled=True, axis_index_groups=near
    )
    return lax.ppermute(spread, "blk", ahead)[None]


def solution(mesh):
    in_specs = (
        P(("grp", "blk"), "sp", None),
        P(("grp", "blk"), "sp", "rep"),
        P(),
        P("sp", "rep"),
        P("sp", "rep"),
        P("rep"),
        P("rep"),
        P("grp"),
    )
    out_specs = P(("grp", "blk"), "sp", "rep")
    return jax.shard_map(
        on_device, mesh=mesh, in_specs=in_specs, out_specs=out_specs, check_vma=False
    )
```

profile of v0, /device:TPU:66, one launch (start us, length us, event | category | flops | bytes accessed | tf_op | source)
XLA Modules:
  0.0 265.2 jit_solution(6549791085957091279)
XLA Ops:
  6.5 0.0 copy-start.1
  6.5 0.0 copy-start.2
  6.6 0.0 all-gather.2.cloned.1.call-start
  6.6 1.1 constant_dynamic-slice_fusion
  7.6 0.7 pad_maximum_fusion
  8.4 0.1 all-gather.2.cloned.1.call-update
  8.4 0.0 copy-start.4
  8.4 0.0 copy-start.5
  8.4 1.5 fusion
  10.0 0.0 copy-done.1
  10.0 0.0 copy-done.2
  10.0 0.3 fusion.2
  10.4 42.3 %collective-permute-start.1 = (bf16[128,2048]{1,0:T(8,128)(2,1)S(1)}, bf16[128,2048]{1,0:T(8,128)(2,1)S(1)}, u32[]{:S(2)}, u32[]{:S(2)}) collective-permute-start(bf16[128,2048]{1,0:T(8,128)(2,1)S(1)} %constant_dynamic-slice_fusion.2), channel_id=1, source_target_pairs={{0,2},{2,0},{4,6},{6,4},{8,10},{10,8},{12,14},{14,12},{1,3},{3,1},... | collective-permute-start | bytes 1572872 | tf_op jit(solution)/shard_map/ppermute | solution.py:253
  52.7 0.0 copy-done.4
  52.7 0.1 dynamic_slice.18
  52.8 0.0 copy-done.5
  52.8 0.1 dynamic_slice.19
  52.9 7.0 %collective-permute-done.1 = bf16[128,2048]{1,0:T(8,128)(2,1)S(1)} collective-permute-done((bf16[128,2048]{1,0:T(8,128)(2,1)S(1)}, bf16[128,2048]{1,0:T(8,128)(2,1)S(1)}, u32[]{:S(2)}, u32[]{:S(2)}) %collective-permute-start.1) | collective-permute-done | bytes 524320 | tf_op jit(solution)/shard_map/ppermute | solution.py:253
  59.9 1.9 collective-permute-start.2
  61.9 0.5 multiply_cosine_fusion
  62.4 1.3 collective-permute-done.2
  63.7 0.1 broadcast_select_fusion.1
  63.8 59.4 %all-gather.2.cloned.1.call-done = bf16[4096,512]{1,0:T(8,128)(2,1)} async-done(((bf16[256,512]{1,0:T(8,128)(2,1)}), bf16[4096,512]{1,0:T(8,128)(2,1)}) %all-gather.2.cloned.1.call-update) | async-done | bytes 4194320 | tf_op jit(solution)/shard_map/all_gather | solution.py:246
  123.2 3.4 %fusion.9 = f32[256,512]{1,0:T(8,128)S(1)} fusion(bf16[4096,512]{1,0:T(8,128)(2,1)} %all-gather.2.cloned.1.call-done, bf16[128,2048]{1,0:T(8,128)(2,1)S(1)} %get-tuple-element.10, bf16[128,2048]{1,0:T(8,128)(2,1)S(1)} %get-tuple-element.9, bf16[128,4096]{1,0:T(8,128)(2,1)S(1)} %fusion.2, f32[512]{0:T(512)S(1)} %maximum_convert_fusion), kind=kOutput, calls=%fused_computation.11 | convolution fusion | flops 1080164352 | bytes 6817792 | tf_op jit(solution)/shard_map/dot_general | solution.py:270
  126.7 0.1 reshape.126
  126.9 0.5 subtract_convert_fusion
  127.4 0.6 pad_maximum_fusion.1
  127.9 0.2 fusion.16
  128.2 2.5 collective-permute-start.3
  130.7 4.3 %collective-permute-done.3 = bf16[128,512]{1,0:T(8,128)(2,1)S(1)} collective-permute-done((bf16[128,512]{1,0:T(8,128)(2,1)S(1)}, bf16[128,512]{1,0:T(8,128)(2,1)S(1)}, u32[]{:S(2)}, u32[]{:S(2)}) %collective-permute-start.3) | collective-permute-done | bytes 131104 | tf_op jit(solution)/shard_map/ppermute | solution.py:295
  135.1 0.2 copy.17
  135.3 0.0 copy-start.3
  135.3 0.1 tile.17
  135.4 27.8 %all_to_all.76 = bf16[128,16,128]{0,2,1:T(8,128)(2,1)S(1)} all-to-all(bf16[128,16,128]{0,2,1:T(8,128)(2,1)S(1)} %bitcast.44), channel_id=1, replica_groups=mesh['grp'=2,'sp'=16,'blk'=8,'rep'=2] {'sp'}, dimensions={1} | all-to-all | bytes 1048576 | tf_op jit(solution)/shard_map/all_to_all | solution.py:303
  163.2 0.9 tile.19
  164.1 5.2 %all-to-all-start.2 = ((bf16[128,16,128]{0,2,1:T(8,128)(2,1)}), bf16[128,16,128]{0,2,1:T(8,128)(2,1)S(1)}, u32[]{:S(2)}, u32[]{:S(2)}) async-start(bf16[128,16,128]{0,2,1:T(8,128)(2,1)} %bitcast.13), calls=%async_computation.2 | async-start | bytes 1048576 | tf_op jit(solution)/shard_map/all_to_all | solution.py:303
  169.3 0.0 copy-done.3
  169.3 2.5 collective-permute-start
  171.8 8.6 %collective-permute-done = bf16[128,2048]{1,0:T(8,128)(2,1)S(1)} collective-permute-done((bf16[128,2048]{1,0:T(8,128)(2,1)S(1)}, bf16[128,2048]{1,0:T(8,128)(2,1)S(1)}, u32[]{:S(2)}, u32[]{:S(2)}) %collective-permute-start) | collective-permute-done | bytes 524320 | tf_op jit(solution)/shard_map/ppermute | solution.py:265
  180.4 0.0 copy-start
  180.4 0.8 copy.23
  181.2 6.4 %all-to-all-done.2 = bf16[128,16,128]{0,2,1:T(8,128)(2,1)S(1)} async-done(((bf16[128,16,128]{0,2,1:T(8,128)(2,1)}), bf16[128,16,128]{0,2,1:T(8,128)(2,1)S(1)}, u32[]{:S(2)}, u32[]{:S(2)}) %all-to-all-start.2) | async-done | bytes 524320 | tf_op jit(solution)/shard_map/all_to_all | solution.py:303
  187.6 7.7 %all-to-all-start = ((bf16[128,4,512]{2,0,1:T(8,128)(2,1)}), bf16[128,4,512]{2,0,1:T(8,128)(2,1)S(1)}, u32[]{:S(2)}, u32[]{:S(2)}) async-start(bf16[128,4,512]{2,0,1:T(8,128)(2,1)} %bitcast.34), calls=%async_computation | async-start | bytes 1048576 | tf_op jit(solution)/shard_map/all_to_all | solution.py:266
  195.3 0.3 copy.13
  195.6 2.6 collective-permute-start.4
  198.2 3.3 %collective-permute-start.5 = (bf16[2048,128]{1,0:T(8,128)(2,1)S(1)}, bf16[2048,128]{1,0:T(8,128)(2,1)S(1)}, u32[]{:S(2)}, u32[]{:S(2)}) collective-permute-start(bf16[2048,128]{1,0:T(8,128)(2,1)S(1)} %bitcast.38), channel_id=1, source_target_pairs={{0,2},{2,4},{4,6},{6,8},{8,10},{10,12},{12,14},{14,0},{1,3},{3,5},... | collective-permute-start | bytes 1572872 | tf_op jit(solution)/shard_map/ppermute | solution.py:308
  201.5 0.3 copy.15
  201.8 3.1 %collective-permute-start.6 = (bf16[2048,128]{1,0:T(8,128)(2,1)S(1)}, bf16[2048,128]{1,0:T(8,128)(2,1)S(1)}, u32[]{:S(2)}, u32[]{:S(2)}) collective-permute-start(bf16[2048,128]{1,0:T(8,128)(2,1)S(1)} %bitcast.40), channel_id=1, source_target_pairs={{2,0},{4,2},{6,4},{8,6},{10,8},{12,10},{14,12},{0,14},{3,1},{5,3},... | collective-permute-start | bytes 1572872 | tf_op jit(solution)/shard_map/ppermute | solution.py:309
  204.9 2.8 %collective-permute-start.7 = (bf16[2048,128]{1,0:T(8,128)(2,1)S(1)}, bf16[2048,128]{1,0:T(8,128)(2,1)}, u32[]{:S(2)}, u32[]{:S(2)}) collective-permute-start(bf16[2048,128]{1,0:T(8,128)(2,1)S(1)} %bitcast.41), channel_id=1, source_target_pairs={{0,2},{2,4},{4,6},{6,8},{8,10},{10,12},{12,14},{14,0},{1,3},{3,5},... | collective-permute-start | bytes 1572872 | tf_op jit(solution)/shard_map/ppermute | solution.py:310
  207.8 0.1 pad_add_fusion.1.info
  207.9 0.1 pad_add_fusion.info
  207.9 0.0 all-to-all-done
  207.9 0.0 copy-done
  207.9 12.4 %attend_first.1 = (f32[4,512,128]{2,1,0:T(8,128)S(1)}, f32[4,512,256]{2,1,0:T(8,128)S(1)}) custom-call(s32[2]{0:T(128)S(1)} %pad_add_fusion.1.info, s32[8]{0:T(128)S(1)} %copy-done, bf16[512,512]{1,0:T(8,128)(2,1)S(1)} %bitcast.35, bf16[2048,128]{1,0:T(8,128)(2,1)S(1)} %bitcast.39, bf16[2048,128]{1,0:T(8,128)(2,1)S(1)} %bitcast.42), custom_call_target="tpu_custom_call" | custom-call | flops 2147483648 | bytes 4194304 | tf_op jit(solution)/shard_map/attend_first/pallas_call | solution.py:195
  220.4 0.0 collective-permute-done.4.refs_0_
  220.4 0.0 collective-permute-done.5.refs_1_
  220.4 0.0 collective-permute-done.6.refs_2_
  220.4 0.0 collective-permute-done.7.refs_3_
  220.4 10.8 %attend_last.1 = bf16[512,512]{1,0:T(8,128)(2,1)S(1)} custom-call(s32[3]{0:T(128)S(1)} %pad_add_fusion.info, s32[8]{0:T(128)S(1)} %copy-done, bf16[512,512]{1,0:T(8,128)(2,1)S(1)} %bitcast.36, bf16[2048,128]{1,0:T(8,128)(2,1)S(1)} %collective-permute-done.4.refs_0_, bf16[2048,128]{1,0:T(8,128)(2,1)S(1)} %collective-permute-done.5.refs_1_, ...), custom_call_target="tpu_custom_call" | custom-call | flops 4294967296 | bytes 4194304 | tf_op jit(solution)/shard_map/attend_last/pallas_call | solution.py:195
  231.2 15.2 %all_to_all.77 = bf16[4,128,512]{2,1,0:T(8,128)(2,1)S(1)} all-to-all(bf16[4,128,512]{2,1,0:T(8,128)(2,1)S(1)} %bitcast.43), channel_id=1, replica_groups={{0,16,32,48},{64,80,96,112},{128,144,160,176},{192,208,224,240},{1,17,3..., dimensions={0} | all-to-all | bytes 1048576 | tf_op jit(solution)/shard_map/all_to_all | solution.py:327
  246.4 2.0 collective-permute-start.8
  248.4 9.1 %collective-permute-done.8 = bf16[128,2048]{1,0:T(8,128)(2,1)S(1)} collective-permute-done((bf16[128,2048]{1,0:T(8,128)(2,1)S(1)}, bf16[128,2048]{1,0:T(8,128)(2,1)S(1)}, u32[]{:S(2)}, u32[]{:S(2)}) %collective-permute-start.8) | collective-permute-done | bytes 524320 | tf_op jit(solution)/shard_map/ppermute | solution.py:330
  257.5 0.8 copy.25
  (15 shorter events, 0.3 us)
Async XLA Ops:
  6.5 3.4 %copy-start.1 = (bf16[1,128,4096]{2,1,0:T(8,128)(2,1)S(1)}, bf16[1,128,4096]{2,1,0:T(8,128)(2,1)}, u32[]{:S(2)}) copy-start(bf16[1,128,4096]{2,1,0:T(8,128)(2,1)} %param.8) | copy-start | bytes 3145732
  6.5 3.4 %copy-start.2 = (f32[4096]{0:T(1024)S(1)}, f32[4096]{0:T(1024)}, u32[]{:S(2)}) copy-start(f32[4096]{0:T(1024)} %param.10) | copy-start | bytes 49156
  6.6 116.6 %all-gather.2.cloned.1.call-start = ((), (), s32[]{:S(2)}) async-start(), calls=%async_computation.4 | async-start | bytes 4456448 | tf_op jit(solution)/shard_map/all_gather | solution.py:246
  8.4 44.3 %copy-start.4 = (bf16[512]{0:T(512)(128)(2,1)S(1)}, bf16[512]{0:T(512)(128)(2,1)}, u32[]{:S(2)}) copy-start(bf16[512]{0:T(512)(128)(2,1)} %param.13) | copy-start | bytes 3076
  8.4 44.4 %copy-start.5 = (bf16[512]{0:T(512)(128)(2,1)S(1)}, bf16[512]{0:T(512)(128)(2,1)}, u32[]{:S(2)}) copy-start(bf16[512]{0:T(512)(128)(2,1)} %param.14) | copy-start | bytes 3076
  10.4 49.5 %collective-permute-start.1 = (bf16[128,2048]{1,0:T(8,128)(2,1)S(1)}, bf16[128,2048]{1,0:T(8,128)(2,1)S(1)}, u32[]{:S(2)}, u32[]{:S(2)}) collective-permute-start(bf16[128,2048]{1,0:T(8,128)(2,1)S(1)} %constant_dynamic-slice_fusion.2), channel_id=1, source_target_pairs={{0,2},{2,0},{4,6},{6,4},{8,10},{10,8},{12,14},{14,12},{1,3},{3,1},... | collective-permute-start | bytes 1572872 | tf_op jit(solution)/shard_map/ppermute | solution.py:253
  59.9 3.8 %collective-permute-start.2 = (bf16[128,2048]{1,0:T(8,128)(2,1)S(1)}, bf16[128,2048]{1,0:T(8,128)(2,1)S(1)}, u32[]{:S(2)}, u32[]{:S(2)}) collective-permute-start(bf16[128,2048]{1,0:T(8,128)(2,1)S(1)} %collective-permute-done.1), channel_id=1, source_target_pairs={{0,1},{1,0},{2,3},{3,2},{4,5},{5,4},{6,7},{7,6},{8,9},{9,8},{10,11... | collective-permute-start | bytes 1572872 | tf_op jit(solution)/shard_map/ppermute | solution.py:254
  128.2 6.9 %collective-permute-start.3 = (bf16[128,512]{1,0:T(8,128)(2,1)S(1)}, bf16[128,512]{1,0:T(8,128)(2,1)S(1)}, u32[]{:S(2)}, u32[]{:S(2)}) collective-permute-start(bf16[128,512]{1,0:T(8,128)(2,1)S(1)} %bitcast.57), channel_id=1, source_target_pairs={{0,2},{2,0},{4,6},{6,4},{8,10},{10,8},{12,14},{14,12},{1,3},{3,1},... | collective-permute-start | bytes 393224 | tf_op jit(solution)/shard_map/ppermute | solution.py:295
  135.3 34.0 %copy-start.3 = (bf16[1,128,2048]{2,1,0:T(8,128)(2,1)S(1)}, bf16[1,128,2048]{2,1,0:T(8,128)(2,1)}, u32[]{:S(2)}) copy-start(bf16[1,128,2048]{2,1,0:T(8,128)(2,1)} %param.9) | copy-start | bytes 1572868
  164.1 23.5 %all-to-all-start.2 = ((bf16[128,16,128]{0,2,1:T(8,128)(2,1)}), bf16[128,16,128]{0,2,1:T(8,128)(2,1)S(1)}, u32[]{:S(2)}, u32[]{:S(2)}) async-start(bf16[128,16,128]{0,2,1:T(8,128)(2,1)} %bitcast.13), calls=%async_computation.2 | async-start | bytes 1048576 | tf_op jit(solution)/shard_map/all_to_all | solution.py:303
  169.3 11.1 %collective-permute-start = (bf16[128,2048]{1,0:T(8,128)(2,1)S(1)}, bf16[128,2048]{1,0:T(8,128)(2,1)S(1)}, u32[]{:S(2)}, u32[]{:S(2)}) collective-permute-start(bf16[128,2048]{1,0:T(8,128)(2,1)S(1)} %bitcast.58), channel_id=1, source_target_pairs={{2,0},{4,2},{6,4},{8,6},{10,8},{12,10},{14,12},{0,14},{3,1},{5,3},... | collective-permute-start | bytes 1572872 | tf_op jit(solution)/shard_map/ppermute | solution.py:265
  180.4 27.6 %copy-start = (s32[8]{0:T(128)S(1)}, s32[8]{0:T(128)}, u32[]{:S(2)}) copy-start(s32[8]{0:T(128)} %docs.3) | copy-start | bytes 100
  187.6 20.3 %all-to-all-start = ((bf16[128,4,512]{2,0,1:T(8,128)(2,1)}), bf16[128,4,512]{2,0,1:T(8,128)(2,1)S(1)}, u32[]{:S(2)}, u32[]{:S(2)}) async-start(bf16[128,4,512]{2,0,1:T(8,128)(2,1)} %bitcast.34), calls=%async_computation | async-start | bytes 1048576 | tf_op jit(solution)/shard_map/all_to_all | solution.py:266
  195.6 24.8 %collective-permute-start.4 = (bf16[2048,128]{1,0:T(8,128)(2,1)S(1)}, bf16[2048,128]{1,0:T(8,128)(2,1)S(1)}, u32[]{:S(2)}, u32[]{:S(2)}) collective-permute-start(bf16[2048,128]{1,0:T(8,128)(2,1)S(1)} %bitcast.37), channel_id=1, source_target_pairs={{2,0},{4,2},{6,4},{8,6},{10,8},{12,10},{14,12},{0,14},{3,1},{5,3},... | collective-permute-start | bytes 1572872 | tf_op jit(solution)/shard_map/ppermute | solution.py:307
  198.2 22.1 %collective-permute-start.5 = (bf16[2048,128]{1,0:T(8,128)(2,1)S(1)}, bf16[2048,128]{1,0:T(8,128)(2,1)S(1)}, u32[]{:S(2)}, u32[]{:S(2)}) collective-permute-start(bf16[2048,128]{1,0:T(8,128)(2,1)S(1)} %bitcast.38), channel_id=1, source_target_pairs={{0,2},{2,4},{4,6},{6,8},{8,10},{10,12},{12,14},{14,0},{1,3},{3,5},... | collective-permute-start | bytes 1572872 | tf_op jit(solution)/shard_map/ppermute | solution.py:308
  201.8 18.6 %collective-permute-start.6 = (bf16[2048,128]{1,0:T(8,128)(2,1)S(1)}, bf16[2048,128]{1,0:T(8,128)(2,1)S(1)}, u32[]{:S(2)}, u32[]{:S(2)}) collective-permute-start(bf16[2048,128]{1,0:T(8,128)(2,1)S(1)} %bitcast.40), channel_id=1, source_target_pairs={{2,0},{4,2},{6,4},{8,6},{10,8},{12,10},{14,12},{0,14},{3,1},{5,3},... | collective-permute-start | bytes 1572872 | tf_op jit(solution)/shard_map/ppermute | solution.py:309
  204.9 15.5 %collective-permute-start.7 = (bf16[2048,128]{1,0:T(8,128)(2,1)S(1)}, bf16[2048,128]{1,0:T(8,128)(2,1)}, u32[]{:S(2)}, u32[]{:S(2)}) collective-permute-start(bf16[2048,128]{1,0:T(8,128)(2,1)S(1)} %bitcast.41), channel_id=1, source_target_pairs={{0,2},{2,4},{4,6},{6,8},{8,10},{10,12},{12,14},{14,0},{1,3},{3,5},... | collective-permute-start | bytes 1572872 | tf_op jit(solution)/shard_map/ppermute | solution.py:310
  246.4 11.1 %collective-permute-start.8 = (bf16[128,2048]{1,0:T(8,128)(2,1)S(1)}, bf16[128,2048]{1,0:T(8,128)(2,1)S(1)}, u32[]{:S(2)}, u32[]{:S(2)}) collective-permute-start(bf16[128,2048]{1,0:T(8,128)(2,1)S(1)} %bitcast.50), channel_id=1, source_target_pairs={{0,2},{2,4},{4,6},{6,8},{8,10},{10,12},{12,14},{14,0},{1,3},{3,5},... | collective-permute-start | bytes 1572872 | tf_op jit(solution)/shard_map/ppermute | solution.py:330
Sparse Core Ops, SparseCore 0:
  9.4 113.7 all-gather.1
where the time goes:
time: 268 us; the launch traced here: 265 us
  waiting for transfers between devices  96.3 us (36%)
  starting transfers between devices  75.9 us (28%)
  blocking collectives  43 us (16%)
  Pallas kernels  23.2 us (9%)
  between operations  13.8 us (5%)
  local copies, waits for them, and re-layouts  5.15 us (2%)
  other arithmetic  4.46 us (2%)
  matrix products  3.43 us (1%)
    all_gather x1, waiting for transfers between devices, on_device(): weight = lax.all_gather(picked, 'sp', axis=0, tiled=True)  59.4 us
    ppermute x1, starting transfers between devices, on_device(): theirs = lax.ppermute(mine, 'blk', swap)  42.3 us
    all_to_all x1, blocking collectives, to_heads(): return lax.all_to_all(sent, 'sp', split_axis=1, concat_axis=0, tiled=True)  27.8 us
    pallas_call x2, Pallas kernels, attend(): pl.pallas_call(functools.partial(attention_kernel, blocks, heads, first,...  23.2 us
    all_to_all x1, blocking collectives, on_device(): lax.all_to_all(result, 'sp', split_axis=0, concat_axis=1, tiled=True, axi...  15.2 us
    ppermute x1, waiting for transfers between devices, on_device(): return lax.ppermute(spread, 'blk', ahead)[None]  9.15 us
    ppermute x1, waiting for transfers between devices, on_device(): query_moved = lax.ppermute(queries[0], 'blk', behind)  8.61 us
    all_to_all x1, starting transfers between devices, on_device(): lax.all_to_all(query_moved, 'sp', split_axis=1, concat_axis=0, tiled=True...  7.68 us
  transfers between devices with their start and end apart: 12, of which 7 were waited for; matrix products, arithmetic and copies ran while one was open for 2% of the time, Pallas kernels for 5%

commit v1 on v0

--- a/solution.py
+++ b/solution.py
@@ -267,6 +267,7 @@
         query_moved, "sp", split_axis=1, concat_axis=0, tiled=True, axis_index_groups=near
     )
 
+    both, query = lax.optimization_barrier((both, query))
     projected = jnp.dot(both, weight, preferred_element_type=jnp.float32)
     bias = jnp.concatenate(
         [

time: 268 us -> 262 us (0.978)
  the two profiles are of different devices: /device:TPU:66 before, /device:TPU:80 now
where the time goes in v1:
time: 262 us; the launch traced here: 260 us
  waiting for transfers between devices  121 us (46%)
  starting transfers between devices  50 us (19%)
  blocking collectives  41.5 us (16%)
  Pallas kernels  17.8 us (7%)
  between operations  13.8 us (5%)
  other arithmetic  5.95 us (2%)
  local copies, waits for them, and re-layouts  5.13 us (2%)
  matrix products  4.06 us (2%)
    all_gather x1, waiting for transfers between devices, on_device(): weight = lax.all_gather(picked, 'sp', axis=0, tiled=True)  77.7 us
    all_to_all x1, blocking collectives, to_heads(): return lax.all_to_all(sent, 'sp', split_axis=1, concat_axis=0, tiled=True)  27.1 us
    pallas_call x2, Pallas kernels, attend(): pl.pallas_call(functools.partial(attention_kernel, blocks, heads, first,...  17.8 us
    all_to_all x1, blocking collectives, on_device(): lax.all_to_all(result, 'sp', split_axis=0, concat_axis=1, tiled=True, axi...  14.4 us
    all_to_all x1, starting transfers between devices, on_device(): lax.all_to_all(query_moved, 'sp', split_axis=1, concat_axis=0, tiled=True...  12.4 us
    all_to_all x1, waiting for transfers between devices, to_heads(): return lax.all_to_all(sent, 'sp', split_axis=1, concat_axis=0, tiled=True)  12.4 us
    ppermute x1, waiting for transfers between devices, on_device(): return lax.ppermute(spread, 'blk', ahead)[None]  10.4 us
    ppermute x1, starting transfers between devices, on_device(): value_next = lax.ppermute(value_block, 'blk', behind)  8.52 us
  transfers between devices with their start and end apart: 12, of which 7 were waited for; matrix products, arithmetic and copies ran while one was open for 2% of the time, Pallas kernels for 5%

profile of v1, /device:TPU:80, one launch (start us, length us, event | category | flops | bytes accessed | tf_op | source)
XLA Modules:
  0.0 259.6 jit_solution(6930924298246702467)
XLA Ops:
  6.5 0.0 copy-start.1
  6.5 0.0 copy-start.2
  6.6 0.0 all-gather.2.cloned.1.call-start
  6.6 1.1 constant_dynamic-slice_fusion
  7.6 0.7 pad_maximum_fusion
  8.4 0.1 all-gather.2.cloned.1.call-update
  8.4 5.8 %collective-permute-start.2 = (bf16[128,2048]{1,0:T(8,128)(2,1)}, bf16[128,2048]{1,0:T(8,128)(2,1)S(1)}, u32[]{:S(2)}, u32[]{:S(2)}) collective-permute-start(bf16[128,2048]{1,0:T(8,128)(2,1)} %bitcast.59), channel_id=1, source_target_pairs={{2,0},{4,2},{6,4},{8,6},{10,8},{12,10},{14,12},{0,14},{3,1},{5,3},... | collective-permute-start | bytes 1572872 | tf_op jit(solution)/shard_map/ppermute | solution.py:265
  14.2 1.5 fusion
  15.7 0.0 copy-done.1
  15.7 0.0 copy-done.2
  15.7 0.3 fusion.2
  16.1 0.0 copy-start.3
  16.1 0.0 copy-start.4
  16.1 2.0 collective-permute-start
  18.1 7.6 %collective-permute-done.2 = bf16[128,2048]{1,0:T(8,128)(2,1)S(1)} collective-permute-done((bf16[128,2048]{1,0:T(8,128)(2,1)}, bf16[128,2048]{1,0:T(8,128)(2,1)S(1)}, u32[]{:S(2)}, u32[]{:S(2)}) %collective-permute-start.2) | collective-permute-done | bytes 524320 | tf_op jit(solution)/shard_map/ppermute | solution.py:265
  25.7 0.8 copy.23
  26.6 12.4 %all-to-all-start = ((bf16[128,4,512]{2,0,1:T(8,128)(2,1)}), bf16[128,4,512]{2,0,1:T(8,128)(2,1)S(1)}, u32[]{:S(2)}, u32[]{:S(2)}) async-start(bf16[128,4,512]{2,0,1:T(8,128)(2,1)} %bitcast.35), calls=%async_computation | async-start | bytes 1048576 | tf_op jit(solution)/shard_map/all_to_all | solution.py:266
  39.0 0.0 copy-done.3
  39.0 0.1 dynamic_slice.19
  39.1 0.0 copy-done.4
  39.1 0.1 dynamic_slice.18
  39.2 0.0 collective-permute-done
  39.2 1.9 collective-permute-start.1
  41.2 0.5 multiply_cosine_fusion
  41.7 1.3 collective-permute-done.1
  43.0 0.1 broadcast_select_fusion.1
  43.1 1.5 maximum_maximum_fusion
  44.6 8.1 %all-to-all-done = bf16[128,4,512]{2,0,1:T(8,128)(2,1)S(1)} async-done(((bf16[128,4,512]{2,0,1:T(8,128)(2,1)}), bf16[128,4,512]{2,0,1:T(8,128)(2,1)S(1)}, u32[]{:S(2)}, u32[]{:S(2)}) %all-to-all-start) | async-done | bytes 524320 | tf_op jit(solution)/shard_map/all_to_all | solution.py:266
  52.7 77.7 %all-gather.2.cloned.1.call-done = bf16[4096,512]{1,0:T(8,128)(2,1)} async-done(((bf16[256,512]{1,0:T(8,128)(2,1)}), bf16[4096,512]{1,0:T(8,128)(2,1)}) %all-gather.2.cloned.1.call-update) | async-done | bytes 4194320 | tf_op jit(solution)/shard_map/all_gather | solution.py:246
  130.4 4.1 %convolution_add_fusion = f32[256,512]{1,0:T(8,128)S(1)} fusion(bf16[256,4096]{1,0:T(8,128)(2,1)} %maximum_maximum_fusion, bf16[4096,512]{1,0:T(8,128)(2,1)} %all-gather.2.cloned.1.call-done, f32[512]{0:T(512)S(1)} %maximum_convert_fusion), kind=kOutput, calls=%fused_computation.6 | convolution fusion | flops 1073872896 | bytes 6817792 | tf_op jit(solution)/shard_map/dot_general | solution.py:271
  134.6 0.1 reshape.126
  134.7 0.5 subtract_convert_fusion
  135.2 0.6 pad_maximum_fusion.1
  135.8 0.2 fusion.6
  136.0 3.1 %collective-permute-start.3 = (bf16[128,512]{1,0:T(8,128)(2,1)S(1)}, bf16[128,512]{1,0:T(8,128)(2,1)S(1)}, u32[]{:S(2)}, u32[]{:S(2)}) collective-permute-start(bf16[128,512]{1,0:T(8,128)(2,1)S(1)} %bitcast.58), channel_id=1, source_target_pairs={{0,2},{2,0},{4,6},{6,4},{8,10},{10,8},{12,14},{14,12},{1,3},{3,1},... | collective-permute-start | bytes 393224 | tf_op jit(solution)/shard_map/ppermute | solution.py:296
  139.1 3.7 %collective-permute-done.3 = bf16[128,512]{1,0:T(8,128)(2,1)S(1)} collective-permute-done((bf16[128,512]{1,0:T(8,128)(2,1)S(1)}, bf16[128,512]{1,0:T(8,128)(2,1)S(1)}, u32[]{:S(2)}, u32[]{:S(2)}) %collective-permute-start.3) | collective-permute-done | bytes 131104 | tf_op jit(solution)/shard_map/ppermute | solution.py:296
  142.9 0.2 copy.17
  143.1 0.1 tile.17
  143.2 27.1 %all_to_all.76 = bf16[128,16,128]{0,2,1:T(8,128)(2,1)S(1)} all-to-all(bf16[128,16,128]{0,2,1:T(8,128)(2,1)S(1)} %bitcast.45), channel_id=1, replica_groups=mesh['grp'=2,'sp'=16,'blk'=8,'rep'=2] {'sp'}, dimensions={1} | all-to-all | bytes 1048576 | tf_op jit(solution)/shard_map/all_to_all | solution.py:304
  170.3 0.0 copy-start
  170.3 0.9 tile.19
  171.2 5.0 %all-to-all-start.2 = ((bf16[128,16,128]{0,2,1:T(8,128)(2,1)}), bf16[128,16,128]{0,2,1:T(8,128)(2,1)S(1)}, u32[]{:S(2)}, u32[]{:S(2)}) async-start(bf16[128,16,128]{0,2,1:T(8,128)(2,1)} %bitcast.13), calls=%async_computation.2 | async-start | bytes 1048576 | tf_op jit(solution)/shard_map/all_to_all | solution.py:304
  176.2 0.3 copy.13
  176.5 5.5 %collective-permute-start.4 = (bf16[2048,128]{1,0:T(8,128)(2,1)S(1)}, bf16[2048,128]{1,0:T(8,128)(2,1)S(1)}, u32[]{:S(2)}, u32[]{:S(2)}) collective-permute-start(bf16[2048,128]{1,0:T(8,128)(2,1)S(1)} %bitcast.38), channel_id=1, source_target_pairs={{2,0},{4,2},{6,4},{8,6},{10,8},{12,10},{14,12},{0,14},{3,1},{5,3},... | collective-permute-start | bytes 1572872 | tf_op jit(solution)/shard_map/ppermute | solution.py:308
  182.0 2.0 collective-permute-start.5
  183.9 12.4 %all-to-all-done.2 = bf16[128,16,128]{0,2,1:T(8,128)(2,1)S(1)} async-done(((bf16[128,16,128]{0,2,1:T(8,128)(2,1)}), bf16[128,16,128]{0,2,1:T(8,128)(2,1)S(1)}, u32[]{:S(2)}, u32[]{:S(2)}) %all-to-all-start.2) | async-done | bytes 524320 | tf_op jit(solution)/shard_map/all_to_all | solution.py:304
  196.4 0.3 copy.15
  196.7 8.5 %collective-permute-start.6 = (bf16[2048,128]{1,0:T(8,128)(2,1)S(1)}, bf16[2048,128]{1,0:T(8,128)(2,1)S(1)}, u32[]{:S(2)}, u32[]{:S(2)}) collective-permute-start(bf16[2048,128]{1,0:T(8,128)(2,1)S(1)} %bitcast.41), channel_id=1, source_target_pairs={{2,0},{4,2},{6,4},{8,6},{10,8},{12,10},{14,12},{0,14},{3,1},{5,3},... | collective-permute-start | bytes 1572872 | tf_op jit(solution)/shard_map/ppermute | solution.py:310
  205.2 2.0 collective-permute-start.7
  207.2 0.1 pad_add_fusion.1.info
  207.2 0.1 pad_add_fusion.info
  207.3 0.0 copy-done
  207.3 12.7 %attend_first.1 = (f32[4,512,128]{2,1,0:T(8,128)S(1)}, f32[4,512,256]{2,1,0:T(8,128)S(1)}) custom-call(s32[2]{0:T(128)S(1)} %pad_add_fusion.1.info, s32[8]{0:T(128)S(1)} %copy-done, bf16[512,512]{1,0:T(8,128)(2,1)S(1)} %bitcast.36, bf16[2048,128]{1,0:T(8,128)(2,1)S(1)} %bitcast.40, bf16[2048,128]{1,0:T(8,128)(2,1)S(1)} %bitcast.43), custom_call_target="tpu_custom_call" | custom-call | flops 2147483648 | bytes 4194304 | tf_op jit(solution)/shard_map/attend_first/pallas_call | solution.py:195
  220.0 0.0 collective-permute-done.4.refs_0_
  220.0 0.0 collective-permute-done.5.refs_1_
  220.0 0.0 collective-permute-done.6.refs_2_
  220.1 0.0 collective-permute-done.7.refs_3_
  220.1 5.1 %attend_last.1 = bf16[512,512]{1,0:T(8,128)(2,1)S(1)} custom-call(s32[3]{0:T(128)S(1)} %pad_add_fusion.info, s32[8]{0:T(128)S(1)} %copy-done, bf16[512,512]{1,0:T(8,128)(2,1)S(1)} %bitcast.37, bf16[2048,128]{1,0:T(8,128)(2,1)S(1)} %collective-permute-done.4.refs_0_, bf16[2048,128]{1,0:T(8,128)(2,1)S(1)} %collective-permute-done.5.refs_1_, ...), custom_call_target="tpu_custom_call" | custom-call | flops 4294967296 | bytes 4194304 | tf_op jit(solution)/shard_map/attend_last/pallas_call | solution.py:195
  225.2 14.4 %all_to_all.77 = bf16[4,128,512]{2,1,0:T(8,128)(2,1)S(1)} all-to-all(bf16[4,128,512]{2,1,0:T(8,128)(2,1)S(1)} %bitcast.44), channel_id=1, replica_groups={{0,16,32,48},{64,80,96,112},{128,144,160,176},{192,208,224,240},{1,17,3..., dimensions={0} | all-to-all | bytes 1048576 | tf_op jit(solution)/shard_map/all_to_all | solution.py:328
  239.6 2.0 collective-permute-start.8
  241.6 10.4 %collective-permute-done.8 = bf16[128,2048]{1,0:T(8,128)(2,1)S(1)} collective-permute-done((bf16[128,2048]{1,0:T(8,128)(2,1)S(1)}, bf16[128,2048]{1,0:T(8,128)(2,1)S(1)}, u32[]{:S(2)}, u32[]{:S(2)}) %collective-permute-start.8) | collective-permute-done | bytes 524320 | tf_op jit(solution)/shard_map/ppermute | solution.py:331
  251.9 0.8 copy.25
  (15 shorter events, 0.3 us)
Async XLA Ops:
  6.5 9.2 %copy-start.1 = (bf16[1,128,4096]{2,1,0:T(8,128)(2,1)S(1)}, bf16[1,128,4096]{2,1,0:T(8,128)(2,1)}, u32[]{:S(2)}) copy-start(bf16[1,128,4096]{2,1,0:T(8,128)(2,1)} %param.8) | copy-start | bytes 3145732
  6.5 9.2 %copy-start.2 = (f32[4096]{0:T(1024)S(1)}, f32[4096]{0:T(1024)}, u32[]{:S(2)}) copy-start(f32[4096]{0:T(1024)} %param.10) | copy-start | bytes 49156
  6.6 123.8 %all-gather.2.cloned.1.call-start = ((), (), s32[]{:S(2)}) async-start(), calls=%async_computation.4 | async-start | bytes 4456448 | tf_op jit(solution)/shard_map/all_gather | solution.py:246
  8.4 17.3 %collective-permute-start.2 = (bf16[128,2048]{1,0:T(8,128)(2,1)}, bf16[128,2048]{1,0:T(8,128)(2,1)S(1)}, u32[]{:S(2)}, u32[]{:S(2)}) collective-permute-start(bf16[128,2048]{1,0:T(8,128)(2,1)} %bitcast.59), channel_id=1, source_target_pairs={{2,0},{4,2},{6,4},{8,6},{10,8},{12,10},{14,12},{0,14},{3,1},{5,3},... | collective-permute-start | bytes 1572872 | tf_op jit(solution)/shard_map/ppermute | solution.py:265
  16.1 22.9 %copy-start.3 = (bf16[512]{0:T(512)(128)(2,1)S(1)}, bf16[512]{0:T(512)(128)(2,1)}, u32[]{:S(2)}) copy-start(bf16[512]{0:T(512)(128)(2,1)} %param.14) | copy-start | bytes 3076
  16.1 23.0 %copy-start.4 = (bf16[512]{0:T(512)(128)(2,1)S(1)}, bf16[512]{0:T(512)(128)(2,1)}, u32[]{:S(2)}) copy-start(bf16[512]{0:T(512)(128)(2,1)} %param.13) | copy-start | bytes 3076
  16.1 23.0 %collective-permute-start = (bf16[128,2048]{1,0:T(8,128)(2,1)S(1)}, bf16[128,2048]{1,0:T(8,128)(2,1)S(1)}, u32[]{:S(2)}, u32[]{:S(2)}) collective-permute-start(bf16[128,2048]{1,0:T(8,128)(2,1)S(1)} %constant_dynamic-slice_fusion.2), channel_id=1, source_target_pairs={{0,2},{2,0},{4,6},{6,4},{8,10},{10,8},{12,14},{14,12},{1,3},{3,1},... | collective-permute-start | bytes 1572872 | tf_op jit(solution)/shard_map/ppermute | solution.py:253
  26.6 26.1 %all-to-all-start = ((bf16[128,4,512]{2,0,1:T(8,128)(2,1)}), bf16[128,4,512]{2,0,1:T(8,128)(2,1)S(1)}, u32[]{:S(2)}, u32[]{:S(2)}) async-start(bf16[128,4,512]{2,0,1:T(8,128)(2,1)} %bitcast.35), calls=%async_computation | async-start | bytes 1048576 | tf_op jit(solution)/shard_map/all_to_all | solution.py:266
  39.2 3.8 %collective-permute-start.1 = (bf16[128,2048]{1,0:T(8,128)(2,1)S(1)}, bf16[128,2048]{1,0:T(8,128)(2,1)S(1)}, u32[]{:S(2)}, u32[]{:S(2)}) collective-permute-start(bf16[128,2048]{1,0:T(8,128)(2,1)S(1)} %collective-permute-done), channel_id=1, source_target_pairs={{0,1},{1,0},{2,3},{3,2},{4,5},{5,4},{6,7},{7,6},{8,9},{9,8},{10,11... | collective-permute-start | bytes 1572872 | tf_op jit(solution)/shard_map/ppermute | solution.py:254
  136.0 6.9 %collective-permute-start.3 = (bf16[128,512]{1,0:T(8,128)(2,1)S(1)}, bf16[128,512]{1,0:T(8,128)(2,1)S(1)}, u32[]{:S(2)}, u32[]{:S(2)}) collective-permute-start(bf16[128,512]{1,0:T(8,128)(2,1)S(1)} %bitcast.58), channel_id=1, source_target_pairs={{0,2},{2,0},{4,6},{6,4},{8,10},{10,8},{12,14},{14,12},{1,3},{3,1},... | collective-permute-start | bytes 393224 | tf_op jit(solution)/shard_map/ppermute | solution.py:296
  170.3 37.0 %copy-start = (s32[8]{0:T(128)S(1)}, s32[8]{0:T(128)}, u32[]{:S(2)}) copy-start(s32[8]{0:T(128)} %docs.3) | copy-start | bytes 100
  171.2 25.2 %all-to-all-start.2 = ((bf16[128,16,128]{0,2,1:T(8,128)(2,1)}), bf16[128,16,128]{0,2,1:T(8,128)(2,1)S(1)}, u32[]{:S(2)}, u32[]{:S(2)}) async-start(bf16[128,16,128]{0,2,1:T(8,128)(2,1)} %bitcast.13), calls=%async_computation.2 | async-start | bytes 1048576 | tf_op jit(solution)/shard_map/all_to_all | solution.py:304
  176.5 43.6 %collective-permute-start.4 = (bf16[2048,128]{1,0:T(8,128)(2,1)S(1)}, bf16[2048,128]{1,0:T(8,128)(2,1)S(1)}, u32[]{:S(2)}, u32[]{:S(2)}) collective-permute-start(bf16[2048,128]{1,0:T(8,128)(2,1)S(1)} %bitcast.38), channel_id=1, source_target_pairs={{2,0},{4,2},{6,4},{8,6},{10,8},{12,10},{14,12},{0,14},{3,1},{5,3},... | collective-permute-start | bytes 1572872 | tf_op jit(solution)/shard_map/ppermute | solution.py:308
  182.0 38.1 %collective-permute-start.5 = (bf16[2048,128]{1,0:T(8,128)(2,1)S(1)}, bf16[2048,128]{1,0:T(8,128)(2,1)S(1)}, u32[]{:S(2)}, u32[]{:S(2)}) collective-permute-start(bf16[2048,128]{1,0:T(8,128)(2,1)S(1)} %bitcast.39), channel_id=1, source_target_pairs={{0,2},{2,4},{4,6},{6,8},{8,10},{10,12},{12,14},{14,0},{1,3},{3,5},... | collective-permute-start | bytes 1572872 | tf_op jit(solution)/shard_map/ppermute | solution.py:309
  196.7 23.4 %collective-permute-start.6 = (bf16[2048,128]{1,0:T(8,128)(2,1)S(1)}, bf16[2048,128]{1,0:T(8,128)(2,1)S(1)}, u32[]{:S(2)}, u32[]{:S(2)}) collective-permute-start(bf16[2048,128]{1,0:T(8,128)(2,1)S(1)} %bitcast.41), channel_id=1, source_target_pairs={{2,0},{4,2},{6,4},{8,6},{10,8},{12,10},{14,12},{0,14},{3,1},{5,3},... | collective-permute-start | bytes 1572872 | tf_op jit(solution)/shard_map/ppermute | solution.py:310
  205.2 14.9 %collective-permute-start.7 = (bf16[2048,128]{1,0:T(8,128)(2,1)S(1)}, bf16[2048,128]{1,0:T(8,128)(2,1)}, u32[]{:S(2)}, u32[]{:S(2)}) collective-permute-start(bf16[2048,128]{1,0:T(8,128)(2,1)S(1)} %bitcast.42), channel_id=1, source_target_pairs={{0,2},{2,4},{4,6},{6,8},{8,10},{10,12},{12,14},{14,0},{1,3},{3,5},... | collective-permute-start | bytes 1572872 | tf_op jit(solution)/shard_map/ppermute | solution.py:311
  239.6 12.3 %collective-permute-start.8 = (bf16[128,2048]{1,0:T(8,128)(2,1)S(1)}, bf16[128,2048]{1,0:T(8,128)(2,1)S(1)}, u32[]{:S(2)}, u32[]{:S(2)}) collective-permute-start(bf16[128,2048]{1,0:T(8,128)(2,1)S(1)} %bitcast.52), channel_id=1, source_target_pairs={{0,2},{2,4},{4,6},{6,8},{8,10},{10,12},{12,14},{14,0},{1,3},{3,5},... | collective-permute-start | bytes 1572872 | tf_op jit(solution)/shard_map/ppermute | solution.py:331
Sparse Core Ops, SparseCore 0:
  9.4 120.8 all-gather.1

commit v2 on v1

--- a/solution.py
+++ b/solution.py
@@ -14,8 +14,9 @@
 START_MAX = -1e30
 HIDDEN_SCORE = -3e38
 EXP2_SCALE = math.log2(math.e) / math.sqrt(HEAD)
-PIECE = 512
+PIECE = 1024
 TILE = 128
+LEAD = 2
 ROWS = 256
 
 
@@ -99,10 +100,11 @@
                 key_place = lanes + (key_low + part * HEAD)
                 parts.append((key_place <= row_place) & (key_place >= begin))
             visible = jnp.concatenate(parts, axis=1)
-        for r in range(heads * TILE // ROWS):
-            rows = slice(r * ROWS, (r + 1) * ROWS)
+        chunks = heads * TILE // ROWS
+
+        def scores_of(r):
             scores = lax.dot_general(
-                stacked[i, rows, :],
+                stacked[i, r * ROWS : (r + 1) * ROWS, :],
                 key,
                 (((1,), (1,)), ((), ())),
                 preferred_element_type=jnp.float32,
@@ -115,6 +117,14 @@
                     ],
                     axis=0,
                 )
+            return scores
+
+        ready = [scores_of(r) for r in range(min(LEAD, chunks))]
+        for r in range(chunks):
+            rows = slice(r * ROWS, (r + 1) * ROWS)
+            scores = ready.pop(0)
+            if r + LEAD < chunks:
+                ready.append(scores_of(r + LEAD))
             old_max = max_ref[i, rows, :]
             new_max = jnp.maximum(old_max, jnp.max(scores, axis=1, keepdims=True))
             factor = jnp.exp2((old_max - new_max) * EXP2_SCALE)
@@ -165,8 +175,8 @@
                 ).astype(jnp.bfloat16)
 
 
-def attend(info, docs, query, keys, values, state, last):
-    tokens = query.shape[0]
+def attend(info, docs, query, keys, values, state, last, part=0, parts=1):
+    tokens = query.shape[0] // parts
     heads = query.shape[1] // HEAD
     tiles = tokens // TILE
     blocks = len(keys)
@@ -191,11 +201,19 @@
         )
         out_specs = (vmem, vmem)
     operands = [query, *keys, *values] + ([] if first else list(state))
+    specs = [pl.BlockSpec((tokens, heads * HEAD), lambda _: (part, 0), memory_space=pltpu.VMEM)]
+    specs += [vmem] * (2 * blocks)
+    if not first:
+        specs += [
+            pl.BlockSpec(shape, lambda _: (part, 0, 0), memory_space=pltpu.VMEM)
+            for shape in (max_shape, sum_shape)
+        ]
     pairs = tokens * heads * keys[0].shape[0] * blocks
     return pl.pallas_call(
         functools.partial(attention_kernel, blocks, heads, first, last),
         out_shape=out_shape,
-        in_specs=[smem, smem] + [vmem] * len(operands),
+        grid=(1,),
+        in_specs=[smem, smem] + specs,
         out_specs=out_specs,
         scratch_shapes=scratch,
         name="attend_last" if last else "attend_first",
@@ -314,21 +332,32 @@
     base = query_block * span_rows
     query_base = base + sp_place // kv_local * quad_rows
     info_first = jnp.stack([query_base, base - span_rows]).astype(jnp.int32)
-    info_last = jnp.stack([query_base, base, base - 2 * span_rows]).astype(jnp.int32)
     state = attend(info_first, doc_lengths, query, [key_block], [value_block], None, False)
-    result = attend(
-        info_last,
-        doc_lengths,
-        query,
-        [key_next, key_prior],
-        [value_next, value_prior],
-        state,
-        True,
-    )
+    shares = []
+    for part in range(2):
+        part_base = query_base + part * (quad_rows // 2)
+        info_last = jnp.stack([part_base, base, base - 2 * span_rows]).astype(jnp.int32)
+        share = attend(
+            info_last,
+            doc_lengths,
+            query,
+            [key_next, key_prior],
+            [value_next, value_prior],
+            state,
+            True,
+            part,
+            2,
+        )
+        shares.append(lax.ppermute(share, "blk", ahead))
     spread = lax.all_to_all(
-        result, "sp", split_axis=0, concat_axis=1, tiled=True, axis_index_groups=near
-    )
-    return lax.ppermute(spread, "blk", ahead)[None]
+        jnp.concatenate(shares, axis=0),
+        "sp",
+        split_axis=0,
+        concat_axis=1,
+        tiled=True,
+        axis_index_groups=near,
+    )
+    return spread[None]
 
 
 def solution(mesh):

time: 262 us -> 262 us (level)
  Pallas kernels: 17.8 us -> 11.2 us
  starting transfers between devices: 50 us -> 53.6 us
    pallas_call x2 -> x3, Pallas kernels: 17.8 us -> 11.2 us  [attend(): pl.pallas_call(functools.partial(attention_kernel, blocks, heads, first,...]
    ppermute x1, waiting for transfers between devices: 0.01 us -> 5.92 us  [on_device(): value_prior = lax.ppermute(value_block, 'blk', ahead)]
    ppermute x1 -> x2, waiting for transfers between devices: 10.4 us -> 5.9 us  [on_device(): shares.append(lax.ppermute(share, 'blk', ahead))]
    ppermute x1 -> x2, starting transfers between devices: 1.95 us -> 5.55 us  [on_device(): shares.append(lax.ppermute(share, 'blk', ahead))]
  transfers between devices with their start and end apart: 12 -> 13, of which waited for: 7 -> 9; matrix products, arithmetic and copies ran while one was open for 2% -> 2% of each run, Pallas kernels for 5% -> 3%
where the time goes in v2:
time: 262 us; the launch traced here: 261 us
  waiting for transfers between devices  123 us (47%)
  starting transfers between devices  53.6 us (20%)
  blocking collectives  43.4 us (17%)
  between operations  13.8 us (5%)
  Pallas kernels  11.2 us (4%)
  other arithmetic  6.05 us (2%)
  local copies, waits for them, and re-layouts  5.87 us (2%)
  matrix products  4.06 us (2%)
    all_gather x1, waiting for transfers between devices, on_device(): weight = lax.all_gather(picked, 'sp', axis=0, tiled=True)  77.7 us
    all_to_all x1, blocking collectives, to_heads(): return lax.all_to_all(sent, 'sp', split_axis=1, concat_axis=0, tiled=True)  27.1 us
    all_to_all x1, blocking collectives, on_device(): lax.all_to_all(jnp.concatenate(shares, axis=0), 'sp', split_axis=0, conca...  16.3 us
    all_to_all x1, starting transfers between devices, on_device(): lax.all_to_all(query_moved, 'sp', split_axis=1, concat_axis=0, tiled=True...  12.4 us
    all_to_all x1, waiting for transfers between devices, to_heads(): return lax.all_to_all(sent, 'sp', split_axis=1, concat_axis=0, tiled=True)  12.4 us
    pallas_call x3, Pallas kernels, attend(): pl.pallas_call(functools.partial(attention_kernel, blocks, heads, first,...  11.2 us
    ppermute x1, starting transfers between devices, on_device(): value_next = lax.ppermute(value_block, 'blk', behind)  8.45 us
    all_to_all x1, waiting for transfers between devices, on_device(): lax.all_to_all(query_moved, 'sp', split_axis=1, concat_axis=0, tiled=True...  8.14 us
  transfers between devices with their start and end apart: 13, of which 9 were waited for; matrix products, arithmetic and copies ran while one was open for 2% of the time, Pallas kernels for 3%

profile of v2, /device:TPU:80, one launch (start us, length us, event | category | flops | bytes accessed | tf_op | source)
XLA Modules:
  0.0 260.9 jit_solution(11682548948851100252)
XLA Ops:
  6.6 0.0 all-gather.2.cloned.1.call-start
  6.6 1.1 constant_dynamic-slice_fusion
  7.6 0.7 pad_maximum_fusion.1
  8.3 0.1 all-gather.2.cloned.1.call-update
  8.4 5.8 %collective-permute-start.2 = (bf16[128,2048]{1,0:T(8,128)(2,1)}, bf16[128,2048]{1,0:T(8,128)(2,1)S(1)}, u32[]{:S(2)}, u32[]{:S(2)}) collective-permute-start(bf16[128,2048]{1,0:T(8,128)(2,1)} %bitcast.56), channel_id=1, source_target_pairs={{2,0},{4,2},{6,4},{8,6},{10,8},{12,10},{14,12},{0,14},{3,1},{5,3},... | collective-permute-start | bytes 1572872 | tf_op jit(solution)/shard_map/ppermute | solution.py:283
  14.2 1.5 fusion
  15.7 0.0 copy-done.1
  15.7 0.0 copy-done.2
  15.7 0.3 fusion.2
  16.1 0.0 copy-start.3
  16.1 0.0 copy-start.4
  16.1 2.0 collective-permute-start
  18.1 7.6 %collective-permute-done.2 = bf16[128,2048]{1,0:T(8,128)(2,1)S(1)} collective-permute-done((bf16[128,2048]{1,0:T(8,128)(2,1)}, bf16[128,2048]{1,0:T(8,128)(2,1)S(1)}, u32[]{:S(2)}, u32[]{:S(2)}) %collective-permute-start.2) | collective-permute-done | bytes 524320 | tf_op jit(solution)/shard_map/ppermute | solution.py:283
  25.7 0.8 copy.22
  26.6 12.4 %all-to-all-start = ((bf16[128,4,512]{2,0,1:T(8,128)(2,1)}), bf16[128,4,512]{2,0,1:T(8,128)(2,1)S(1)}, u32[]{:S(2)}, u32[]{:S(2)}) async-start(bf16[128,4,512]{2,0,1:T(8,128)(2,1)} %bitcast.33), calls=%async_computation | async-start | bytes 1048576 | tf_op jit(solution)/shard_map/all_to_all | solution.py:284
  39.0 0.0 copy-done.3
  39.0 0.1 dynamic_slice.19
  39.1 0.0 copy-done.4
  39.1 0.1 dynamic_slice.18
  39.2 0.0 collective-permute-done
  39.2 1.9 collective-permute-start.1
  41.1 0.5 multiply_cosine_fusion
  41.7 1.3 collective-permute-done.1
  43.0 0.1 broadcast_select_fusion.1
  43.1 1.5 maximum_maximum_fusion
  44.5 8.1 %all-to-all-done = bf16[128,4,512]{2,0,1:T(8,128)(2,1)S(1)} async-done(((bf16[128,4,512]{2,0,1:T(8,128)(2,1)}), bf16[128,4,512]{2,0,1:T(8,128)(2,1)S(1)}, u32[]{:S(2)}, u32[]{:S(2)}) %all-to-all-start) | async-done | bytes 524320 | tf_op jit(solution)/shard_map/all_to_all | solution.py:284
  52.7 77.7 %all-gather.2.cloned.1.call-done = bf16[4096,512]{1,0:T(8,128)(2,1)} async-done(((bf16[256,512]{1,0:T(8,128)(2,1)}), bf16[4096,512]{1,0:T(8,128)(2,1)}) %all-gather.2.cloned.1.call-update) | async-done | bytes 4194320 | tf_op jit(solution)/shard_map/all_gather | solution.py:264
  130.4 4.1 %convolution_add_fusion = f32[256,512]{1,0:T(8,128)S(1)} fusion(bf16[256,4096]{1,0:T(8,128)(2,1)} %maximum_maximum_fusion, bf16[4096,512]{1,0:T(8,128)(2,1)} %all-gather.2.cloned.1.call-done, f32[512]{0:T(512)S(1)} %maximum_convert_fusion), kind=kOutput, calls=%fused_computation.6 | convolution fusion | flops 1073872896 | bytes 6817792 | tf_op jit(solution)/shard_map/dot_general | solution.py:289
  134.5 0.1 reshape.127
  134.7 0.5 subtract_convert_fusion
  135.2 0.6 pad_maximum_fusion.2
  135.8 0.2 fusion.6
  136.0 3.0 %collective-permute-start.3 = (bf16[128,512]{1,0:T(8,128)(2,1)S(1)}, bf16[128,512]{1,0:T(8,128)(2,1)S(1)}, u32[]{:S(2)}, u32[]{:S(2)}) collective-permute-start(bf16[128,512]{1,0:T(8,128)(2,1)S(1)} %bitcast.55), channel_id=1, source_target_pairs={{0,2},{2,0},{4,6},{6,4},{8,10},{10,8},{12,14},{14,12},{1,3},{3,1},... | collective-permute-start | bytes 393224 | tf_op jit(solution)/shard_map/ppermute | solution.py:314
  139.0 3.9 %collective-permute-done.3 = bf16[128,512]{1,0:T(8,128)(2,1)S(1)} collective-permute-done((bf16[128,512]{1,0:T(8,128)(2,1)S(1)}, bf16[128,512]{1,0:T(8,128)(2,1)S(1)}, u32[]{:S(2)}, u32[]{:S(2)}) %collective-permute-start.3) | collective-permute-done | bytes 131104 | tf_op jit(solution)/shard_map/ppermute | solution.py:314
  142.9 0.2 copy.17
  143.1 0.1 tile.17
  143.2 27.1 %all_to_all.73 = bf16[128,16,128]{0,2,1:T(8,128)(2,1)S(1)} all-to-all(bf16[128,16,128]{0,2,1:T(8,128)(2,1)S(1)} %bitcast.43), channel_id=1, replica_groups=mesh['grp'=2,'sp'=16,'blk'=8,'rep'=2] {'sp'}, dimensions={1} | all-to-all | bytes 1048576 | tf_op jit(solution)/shard_map/all_to_all | solution.py:322
  170.3 0.9 tile.19
  171.2 5.0 %all-to-all-start.2 = ((bf16[128,16,128]{0,2,1:T(8,128)(2,1)}), bf16[128,16,128]{0,2,1:T(8,128)(2,1)S(1)}, u32[]{:S(2)}, u32[]{:S(2)}) async-start(bf16[128,16,128]{0,2,1:T(8,128)(2,1)} %bitcast.13), calls=%async_computation.2 | async-start | bytes 1048576 | tf_op jit(solution)/shard_map/all_to_all | solution.py:322
  176.2 0.3 copy.13
  176.5 5.5 %collective-permute-start.4 = (bf16[2048,128]{1,0:T(8,128)(2,1)S(1)}, bf16[2048,128]{1,0:T(8,128)(2,1)S(1)}, u32[]{:S(2)}, u32[]{:S(2)}) collective-permute-start(bf16[2048,128]{1,0:T(8,128)(2,1)S(1)} %bitcast.37), channel_id=1, source_target_pairs={{2,0},{4,2},{6,4},{8,6},{10,8},{12,10},{14,12},{0,14},{3,1},{5,3},... | collective-permute-start | bytes 1572872 | tf_op jit(solution)/shard_map/ppermute | solution.py:326
  182.0 2.0 collective-permute-start.5
  184.0 12.4 %all-to-all-done.2 = bf16[128,16,128]{0,2,1:T(8,128)(2,1)S(1)} async-done(((bf16[128,16,128]{0,2,1:T(8,128)(2,1)}), bf16[128,16,128]{0,2,1:T(8,128)(2,1)S(1)}, u32[]{:S(2)}, u32[]{:S(2)}) %all-to-all-start.2) | async-done | bytes 524320 | tf_op jit(solution)/shard_map/all_to_all | solution.py:322
  196.4 0.3 copy.15
  196.7 8.5 %collective-permute-start.6 = (bf16[2048,128]{1,0:T(8,128)(2,1)S(1)}, bf16[2048,128]{1,0:T(8,128)(2,1)S(1)}, u32[]{:S(2)}, u32[]{:S(2)}) collective-permute-start(bf16[2048,128]{1,0:T(8,128)(2,1)S(1)} %bitcast.40), channel_id=1, source_target_pairs={{2,0},{4,2},{6,4},{8,6},{10,8},{12,10},{14,12},{0,14},{3,1},{5,3},... | collective-permute-start | bytes 1572872 | tf_op jit(solution)/shard_map/ppermute | solution.py:328
  205.1 2.1 collective-permute-start.7
  207.3 0.1 add_add_fusion.1.info
  207.4 0.1 add_add_fusion.info
  207.4 0.1 pad_add_fusion.info
  207.5 0.0 copy-done
  207.5 5.2 %attend_first.1 = (f32[4,512,128]{2,1,0:T(8,128)S(1)}, f32[4,512,256]{2,1,0:T(8,128)S(1)}) custom-call(s32[2]{0:T(128)S(1)} %pad_add_fusion.info, s32[8]{0:T(128)S(1)} %copy-done, bf16[512,512]{1,0:T(8,128)(2,1)S(1)} %bitcast.34, bf16[2048,128]{1,0:T(8,128)(2,1)S(1)} %bitcast.39, bf16[2048,128]{1,0:T(8,128)(2,1)S(1)} %bitcast.42), custom_call_target="tpu_custom_call" | custom-call | flops 2147483648 | bytes 4194304 | tf_op jit(solution)/shard_map/attend_first/pallas_call | solution.py:212
  212.7 0.0 collective-permute-done.4.refs_0_
  212.7 0.0 collective-permute-done.5.refs_1_
  212.7 0.0 collective-permute-done.6.refs_2_
  212.8 5.9 %collective-permute-done.7.refs_3_ = bf16[2048,128]{1,0:T(8,128)(2,1)S(1)} collective-permute-done((bf16[2048,128]{1,0:T(8,128)(2,1)S(1)}, bf16[2048,128]{1,0:T(8,128)(2,1)S(1)}, u32[]{:S(2)}, u32[]{:S(2)}) %collective-permute-start.7) | collective-permute-done | bytes 524320 | tf_op jit(solution)/shard_map/ppermute | solution.py:329
  218.7 3.0 %attend_last.3 = bf16[256,512]{1,0:T(8,128)(2,1)S(1)} custom-call(s32[3]{0:T(128)S(1)} %add_add_fusion.1.info, s32[8]{0:T(128)S(1)} %copy-done, bf16[512,512]{1,0:T(8,128)(2,1)S(1)} %bitcast.35, bf16[2048,128]{1,0:T(8,128)(2,1)S(1)} %collective-permute-done.4.refs_0_, bf16[2048,128]{1,0:T(8,128)(2,1)S(1)} %collective-permute-done.5.refs_1_, ...), custom_call_target="tpu_custom_call" | custom-call | flops 2147483648 | bytes 4194304 | tf_op jit(solution)/shard_map/attend_last/pallas_call | solution.py:212
  221.7 2.0 collective-permute-start.9
  223.6 3.0 %attend_last.2 = bf16[256,512]{1,0:T(8,128)(2,1)S(1)} custom-call(s32[3]{0:T(128)S(1)} %add_add_fusion.info, s32[8]{0:T(128)S(1)} %copy-done, bf16[512,512]{1,0:T(8,128)(2,1)S(1)} %bitcast.36, bf16[2048,128]{1,0:T(8,128)(2,1)S(1)} %collective-permute-done.4.refs_0_, bf16[2048,128]{1,0:T(8,128)(2,1)S(1)} %collective-permute-done.5.refs_1_, ...), custom_call_target="tpu_custom_call" | custom-call | flops 2147483648 | bytes 4194304 | tf_op jit(solution)/shard_map/attend_last/pallas_call | solution.py:212
  226.7 3.6 %collective-permute-start.8 = (bf16[256,512]{1,0:T(8,128)(2,1)S(1)}, bf16[256,512]{1,0:T(8,128)(2,1)S(1)}, u32[]{:S(2)}, u32[]{:S(2)}) collective-permute-start(bf16[256,512]{1,0:T(8,128)(2,1)S(1)} %attend_last.2), channel_id=1, source_target_pairs={{0,2},{2,4},{4,6},{6,8},{8,10},{10,12},{12,14},{14,0},{1,3},{3,5},... | collective-permute-start | bytes 786440 | tf_op jit(solution)/shard_map/ppermute | solution.py:351
  230.3 0.9 collective-permute-done.9
  231.2 5.0 %collective-permute-done.8 = bf16[256,512]{1,0:T(8,128)(2,1)S(1)} collective-permute-done((bf16[256,512]{1,0:T(8,128)(2,1)S(1)}, bf16[256,512]{1,0:T(8,128)(2,1)S(1)}, u32[]{:S(2)}, u32[]{:S(2)}) %collective-permute-start.8) | collective-permute-done | bytes 262176 | tf_op jit(solution)/shard_map/ppermute | solution.py:351
  236.2 16.3 %all_to_all.74 = bf16[4,128,512]{2,1,0:T(8,128)(2,1)S(1)} all-to-all(bf16[4,128,512]{2,1,0:T(8,128)(2,1)S(1)} %bitcast.46), channel_id=1, replica_groups={{0,16,32,48},{64,80,96,112},{128,144,160,176},{192,208,224,240},{1,17,3..., dimensions={0} | all-to-all | bytes 1048576 | tf_op jit(solution)/shard_map/all_to_all | solution.py:352
  252.5 0.4 copy.16
  252.9 1.2 broadcast_in_dim.2
  (18 shorter events, 0.3 us)
Async XLA Ops:
  6.5 9.2 %copy-start.1 = (bf16[1,128,4096]{2,1,0:T(8,128)(2,1)S(1)}, bf16[1,128,4096]{2,1,0:T(8,128)(2,1)}, u32[]{:S(2)}) copy-start(bf16[1,128,4096]{2,1,0:T(8,128)(2,1)} %param.8) | copy-start | bytes 3145732
  6.5 9.2 %copy-start.2 = (f32[4096]{0:T(1024)S(1)}, f32[4096]{0:T(1024)}, u32[]{:S(2)}) copy-start(f32[4096]{0:T(1024)} %param.10) | copy-start | bytes 49156
  6.6 123.8 %all-gather.2.cloned.1.call-start = ((), (), s32[]{:S(2)}) async-start(), calls=%async_computation.4 | async-start | bytes 4456448 | tf_op jit(solution)/shard_map/all_gather | solution.py:264
  8.4 17.3 %collective-permute-start.2 = (bf16[128,2048]{1,0:T(8,128)(2,1)}, bf16[128,2048]{1,0:T(8,128)(2,1)S(1)}, u32[]{:S(2)}, u32[]{:S(2)}) collective-permute-start(bf16[128,2048]{1,0:T(8,128)(2,1)} %bitcast.56), channel_id=1, source_target_pairs={{2,0},{4,2},{6,4},{8,6},{10,8},{12,10},{14,12},{0,14},{3,1},{5,3},... | collective-permute-start | bytes 1572872 | tf_op jit(solution)/shard_map/ppermute | solution.py:283
  16.1 22.9 %copy-start.3 = (bf16[512]{0:T(512)(128)(2,1)S(1)}, bf16[512]{0:T(512)(128)(2,1)}, u32[]{:S(2)}) copy-start(bf16[512]{0:T(512)(128)(2,1)} %param.14) | copy-start | bytes 3076
  16.1 23.0 %copy-start.4 = (bf16[512]{0:T(512)(128)(2,1)S(1)}, bf16[512]{0:T(512)(128)(2,1)}, u32[]{:S(2)}) copy-start(bf16[512]{0:T(512)(128)(2,1)} %param.13) | copy-start | bytes 3076
  16.1 23.0 %collective-permute-start = (bf16[128,2048]{1,0:T(8,128)(2,1)S(1)}, bf16[128,2048]{1,0:T(8,128)(2,1)S(1)}, u32[]{:S(2)}, u32[]{:S(2)}) collective-permute-start(bf16[128,2048]{1,0:T(8,128)(2,1)S(1)} %constant_dynamic-slice_fusion.2), channel_id=1, source_target_pairs={{0,2},{2,0},{4,6},{6,4},{8,10},{10,8},{12,14},{14,12},{1,3},{3,1},... | collective-permute-start | bytes 1572872 | tf_op jit(solution)/shard_map/ppermute | solution.py:271
  26.6 26.1 %all-to-all-start = ((bf16[128,4,512]{2,0,1:T(8,128)(2,1)}), bf16[128,4,512]{2,0,1:T(8,128)(2,1)S(1)}, u32[]{:S(2)}, u32[]{:S(2)}) async-start(bf16[128,4,512]{2,0,1:T(8,128)(2,1)} %bitcast.33), calls=%async_computation | async-start | bytes 1048576 | tf_op jit(solution)/shard_map/all_to_all | solution.py:284
  39.2 3.8 %collective-permute-start.1 = (bf16[128,2048]{1,0:T(8,128)(2,1)S(1)}, bf16[128,2048]{1,0:T(8,128)(2,1)S(1)}, u32[]{:S(2)}, u32[]{:S(2)}) collective-permute-start(bf16[128,2048]{1,0:T(8,128)(2,1)S(1)} %collective-permute-done), channel_id=1, source_target_pairs={{0,1},{1,0},{2,3},{3,2},{4,5},{5,4},{6,7},{7,6},{8,9},{9,8},{10,11... | collective-permute-start | bytes 1572872 | tf_op jit(solution)/shard_map/ppermute | solution.py:272
  136.0 6.9 %collective-permute-start.3 = (bf16[128,512]{1,0:T(8,128)(2,1)S(1)}, bf16[128,512]{1,0:T(8,128)(2,1)S(1)}, u32[]{:S(2)}, u32[]{:S(2)}) collective-permute-start(bf16[128,512]{1,0:T(8,128)(2,1)S(1)} %bitcast.55), channel_id=1, source_target_pairs={{0,2},{2,0},{4,6},{6,4},{8,10},{10,8},{12,14},{14,12},{1,3},{3,1},... | collective-permute-start | bytes 393224 | tf_op jit(solution)/shard_map/ppermute | solution.py:314
  170.3 37.2 %copy-start = (s32[8]{0:T(128)S(1)}, s32[8]{0:T(128)}, u32[]{:S(2)}) copy-start(s32[8]{0:T(128)} %docs.5) | copy-start | bytes 100
  171.2 25.2 %all-to-all-start.2 = ((bf16[128,16,128]{0,2,1:T(8,128)(2,1)}), bf16[128,16,128]{0,2,1:T(8,128)(2,1)S(1)}, u32[]{:S(2)}, u32[]{:S(2)}) async-start(bf16[128,16,128]{0,2,1:T(8,128)(2,1)} %bitcast.13), calls=%async_computation.2 | async-start | bytes 1048576 | tf_op jit(solution)/shard_map/all_to_all | solution.py:322
  176.5 36.2 %collective-permute-start.4 = (bf16[2048,128]{1,0:T(8,128)(2,1)S(1)}, bf16[2048,128]{1,0:T(8,128)(2,1)S(1)}, u32[]{:S(2)}, u32[]{:S(2)}) collective-permute-start(bf16[2048,128]{1,0:T(8,128)(2,1)S(1)} %bitcast.37), channel_id=1, source_target_pairs={{2,0},{4,2},{6,4},{8,6},{10,8},{12,10},{14,12},{0,14},{3,1},{5,3},... | collective-permute-start | bytes 1572872 | tf_op jit(solution)/shard_map/ppermute | solution.py:326
  182.0 30.7 %collective-permute-start.5 = (bf16[2048,128]{1,0:T(8,128)(2,1)S(1)}, bf16[2048,128]{1,0:T(8,128)(2,1)S(1)}, u32[]{:S(2)}, u32[]{:S(2)}) collective-permute-start(bf16[2048,128]{1,0:T(8,128)(2,1)S(1)} %bitcast.38), channel_id=1, source_target_pairs={{0,2},{2,4},{4,6},{6,8},{8,10},{10,12},{12,14},{14,0},{1,3},{3,5},... | collective-permute-start | bytes 1572872 | tf_op jit(solution)/shard_map/ppermute | solution.py:327
  196.7 16.1 %collective-permute-start.6 = (bf16[2048,128]{1,0:T(8,128)(2,1)S(1)}, bf16[2048,128]{1,0:T(8,128)(2,1)S(1)}, u32[]{:S(2)}, u32[]{:S(2)}) collective-permute-start(bf16[2048,128]{1,0:T(8,128)(2,1)S(1)} %bitcast.40), channel_id=1, source_target_pairs={{2,0},{4,2},{6,4},{8,6},{10,8},{12,10},{14,12},{0,14},{3,1},{5,3},... | collective-permute-start | bytes 1572872 | tf_op jit(solution)/shard_map/ppermute | solution.py:328
  205.1 13.5 %collective-permute-start.7 = (bf16[2048,128]{1,0:T(8,128)(2,1)S(1)}, bf16[2048,128]{1,0:T(8,128)(2,1)S(1)}, u32[]{:S(2)}, u32[]{:S(2)}) collective-permute-start(bf16[2048,128]{1,0:T(8,128)(2,1)S(1)} %bitcast.41), channel_id=1, source_target_pairs={{0,2},{2,4},{4,6},{6,8},{8,10},{10,12},{12,14},{14,0},{1,3},{3,5},... | collective-permute-start | bytes 1572872 | tf_op jit(solution)/shard_map/ppermute | solution.py:329
  221.7 9.5 %collective-permute-start.9 = (bf16[256,512]{1,0:T(8,128)(2,1)S(1)}, bf16[256,512]{1,0:T(8,128)(2,1)S(1)}, u32[]{:S(2)}, u32[]{:S(2)}) collective-permute-start(bf16[256,512]{1,0:T(8,128)(2,1)S(1)} %attend_last.3), channel_id=1, source_target_pairs={{0,2},{2,4},{4,6},{6,8},{8,10},{10,12},{12,14},{14,0},{1,3},{3,5},... | collective-permute-start | bytes 786440 | tf_op jit(solution)/shard_map/ppermute | solution.py:351
  226.7 9.5 %collective-permute-start.8 = (bf16[256,512]{1,0:T(8,128)(2,1)S(1)}, bf16[256,512]{1,0:T(8,128)(2,1)S(1)}, u32[]{:S(2)}, u32[]{:S(2)}) collective-permute-start(bf16[256,512]{1,0:T(8,128)(2,1)S(1)} %attend_last.2), channel_id=1, source_target_pairs={{0,2},{2,4},{4,6},{6,8},{8,10},{10,12},{12,14},{14,0},{1,3},{3,5},... | collective-permute-start | bytes 786440 | tf_op jit(solution)/shard_map/ppermute | solution.py:351
Sparse Core Ops, SparseCore 0:
  9.4 120.8 all-gather.1

commit v3 on v2

--- a/solution.py
+++ b/solution.py
@@ -20,19 +20,65 @@
 ROWS = 256
 
 
-def apply_rotation(projected, token_places):
-    half_size = projected.shape[-1] // 2
+def rotation(token_places):
+    half_size = HEAD // 2
     freq_index = jnp.arange(half_size).astype(jnp.float32)
-    inverse = jnp.exp(freq_index * (-2.0 * math.log(THETA_BASE) / projected.shape[-1]))
+    inverse = jnp.exp(freq_index * (-2.0 * math.log(THETA_BASE) / HEAD))
     angles = token_places[:, None] * inverse[None, :]
-    cosine = jnp.cos(angles)[:, None, :]
-    sine = jnp.sin(angles)[:, None, :]
-    first_half = projected[..., :half_size]
-    second_half = projected[..., half_size:]
-    return jnp.concatenate(
-        [first_half * cosine - second_half * sine, second_half * cosine + first_half * sine],
-        axis=-1,
-    )
+    cosine = jnp.cos(angles)
+    sine = jnp.sin(angles)
+    return jnp.concatenate([cosine, cosine], axis=1), jnp.concatenate([-sine, sine], axis=1)
+
+
+def project_kernel(heads, tokens_ref, weight_ref, bias_ref, cosine_ref, sine_ref, out_ref, total):
+    step = pl.program_id(0)
+    product = jnp.dot(tokens_ref[...], weight_ref[...], preferred_element_type=jnp.float32)
+
+    @pl.when(step == 0)
+    def _():
+        total[...] = product
+
+    @pl.when(step > 0)
+    def _():
+        total[...] += product
+
+    @pl.when(step == pl.num_programs(0) - 1)
+    def _():
+        for h in range(heads):
+            columns = slice(h * HEAD, (h + 1) * HEAD)
+            key = total[:, columns] + bias_ref[:, columns]
+            turned = key * cosine_ref[...] + pltpu.roll(key, HEAD // 2, 1) * sine_ref[...]
+            out_ref[:, columns] = turned.astype(jnp.bfloat16)
+        rest = slice(heads * HEAD, 2 * heads * HEAD)
+        out_ref[:, rest] = (total[:, rest] + bias_ref[:, rest]).astype(jnp.bfloat16)
+
+
+def project(tokens, weight, bias, cosine, sine):
+    rows, width = tokens.shape
+    columns = weight.shape[1]
+    depth = 1024
+    whole = lambda shape: pl.BlockSpec(shape, lambda k: (0, 0))
+    return pl.pallas_call(
+        functools.partial(project_kernel, columns // (2 * HEAD)),
+        out_shape=jax.ShapeDtypeStruct((rows, columns), jnp.bfloat16),
+        grid=(width // depth,),
+        in_specs=[
+            pl.BlockSpec((rows, depth), lambda k: (0, k)),
+            pl.BlockSpec((depth, columns), lambda k: (k, 0)),
+            whole((1, columns)),
+            whole((rows, HEAD)),
+            whole((rows, HEAD)),
+        ],
+        out_specs=whole((rows, columns)),
+        scratch_shapes=[pltpu.VMEM((rows, columns), jnp.float32)],
+        name="project",
+        cost_estimate=pl.CostEstimate(
+            flops=2 * rows * width * columns,
+            bytes_accessed=2 * (rows + columns) * width,
+            transcendentals=0,
+        ),
+        compiler_params=pltpu.CompilerParams(vmem_limit_bytes=58 << 20),
+    )(tokens, weight, bias, cosine, sine)
 
 
 def attention_kernel(blocks, heads, first, last, info, docs, q_ref, *refs):
@@ -280,46 +326,36 @@
     )
     both = jnp.concatenate([normed, partner], axis=0)
 
-    query_moved = lax.ppermute(queries[0], "blk", behind)
     query = lax.all_to_all(
-        query_moved, "sp", split_axis=1, concat_axis=0, tiled=True, axis_index_groups=near
-    )
-
-    both, query = lax.optimization_barrier((both, query))
-    projected = jnp.dot(both, weight, preferred_element_type=jnp.float32)
+        queries[0], "sp", split_axis=1, concat_axis=0, tiled=True, axis_index_groups=near
+    )
+
     bias = jnp.concatenate(
         [
             lax.dynamic_slice_in_dim(key_shift_bias, side * half_columns, half_columns, 0),
             lax.dynamic_slice_in_dim(value_shift_bias, side * half_columns, half_columns, 0),
         ]
-    ).astype(jnp.float32)
-    projected = projected + bias
+    ).astype(jnp.float32)[None]
     local_places = sp_place * local_rows + jnp.arange(local_rows)
     places = jnp.concatenate(
         [local_places + blk_place * span_rows, local_places + (blk_place ^ 1) * span_rows]
     )
-    keys_new = apply_rotation(
-        projected[:, :half_columns].reshape(2 * local_rows, half_heads, HEAD),
-        places.astype(jnp.float32),
-    ).astype(jnp.bfloat16)
-    values_new = (
-        projected[:, half_columns:]
-        .reshape(2 * local_rows, half_heads, HEAD)
-        .astype(jnp.bfloat16)
-    )
-    pair_new = jnp.concatenate([keys_new, values_new], axis=2).reshape(
-        2 * local_rows, half_heads * 2 * HEAD
-    )
-    kept = pair_new[:local_rows]
-    other = lax.ppermute(pair_new[local_rows:], "blk", swap)
-    even = side == 0
-    all_heads = jnp.concatenate(
-        [jnp.where(even, kept, other), jnp.where(even, other, kept)], axis=1
-    )
+    cosine, sine = rotation(places.astype(jnp.float32))
+    both, query, bias, cosine, sine = lax.optimization_barrier((both, query, bias, cosine, sine))
+    made = project(both, weight, bias, cosine, sine)
+    near_half = lax.ppermute(made[:local_rows], "blk", ahead)
+    far_half = lax.ppermute(
+        made[local_rows:], "blk", [(b, ((b ^ 1) + 1) % blk_count) for b in range(blk_count)]
+    )
+    odd = side == 1
+
     def to_heads(part):
-        one = all_heads.reshape(local_rows, kv_local, 2 * HEAD)[:, :, part * HEAD : (part + 1) * HEAD]
-        sent = jnp.tile(one.reshape(local_rows, kv_local * HEAD), (1, quads))
-        return lax.all_to_all(sent, "sp", split_axis=1, concat_axis=0, tiled=True)
+        columns = slice(part * half_columns, (part + 1) * half_columns)
+        one, two = near_half[:, columns], far_half[:, columns]
+        heads = jnp.concatenate([jnp.where(odd, one, two), jnp.where(odd, two, one)], axis=1)
+        return lax.all_to_all(
+            jnp.tile(heads, (1, quads)), "sp", split_axis=1, concat_axis=0, tiled=True
+        )
 
     key_block = to_heads(0)
     value_block = to_heads(1)
@@ -328,36 +364,29 @@
     value_next = lax.ppermute(value_block, "blk", behind)
     value_prior = lax.ppermute(value_block, "blk", ahead)
 
-    query_block = (blk_place + 1) % blk_count
-    base = query_block * span_rows
+    base = blk_place * span_rows
     query_base = base + sp_place // kv_local * quad_rows
     info_first = jnp.stack([query_base, base - span_rows]).astype(jnp.int32)
+    info_last = jnp.stack([query_base, base, base - 2 * span_rows]).astype(jnp.int32)
     state = attend(info_first, doc_lengths, query, [key_block], [value_block], None, False)
-    shares = []
-    for part in range(2):
-        part_base = query_base + part * (quad_rows // 2)
-        info_last = jnp.stack([part_base, base, base - 2 * span_rows]).astype(jnp.int32)
-        share = attend(
-            info_last,
-            doc_lengths,
-            query,
-            [key_next, key_prior],
-            [value_next, value_prior],
-            state,
-            True,
-            part,
-            2,
-        )
-        shares.append(lax.ppermute(share, "blk", ahead))
+    result = attend(
+        info_last,
+        doc_lengths,
+        query,
+        [key_next, key_prior],
+        [value_next, value_prior],
+        state,
+        True,
+    )
     spread = lax.all_to_all(
-        jnp.concatenate(shares, axis=0),
+        result.reshape(kv_local, local_rows, result.shape[1]),
         "sp",
         split_axis=0,
-        concat_axis=1,
+        concat_axis=0,
         tiled=True,
         axis_index_groups=near,
     )
-    return spread[None]
+    return jnp.concatenate([spread[i] for i in range(kv_local)], axis=1)[None]
 
 
 def solution(mesh):

time: 262 us -> 251 us (0.958)
  the two profiles are of different devices: /device:TPU:80 before, /device:TPU:74 now
where the time goes in v3:
time: 251 us; the launch traced here: 250 us
  waiting for transfers between devices  127 us (51%)
  starting transfers between devices  53.6 us (21%)
  Pallas kernels  27 us (11%)
  blocking collectives  14.4 us (6%)
  between operations  13.7 us (5%)
  other arithmetic  7.89 us (3%)
  local copies, waits for them, and re-layouts  6.17 us (2%)
    all_gather x1, waiting for transfers between devices, on_device(): weight = lax.all_gather(picked, 'sp', axis=0, tiled=True)  84 us
    all_to_all x2, waiting for transfers between devices, to_heads(): lax.all_to_all(jnp.tile(heads, (1, quads)), 'sp', split_axis=1, concat_ax...  31 us
    pallas_call x2, Pallas kernels, attend(): pl.pallas_call(functools.partial(attention_kernel, blocks, heads, first,...  21.7 us
    all_to_all x1, blocking collectives, on_device(): lax.all_to_all(result.reshape(kv_local, local_rows, result.shape[1]), 'sp...  14.4 us
    all_to_all x2, starting transfers between devices, to_heads(): lax.all_to_all(jnp.tile(heads, (1, quads)), 'sp', split_axis=1, concat_ax...  13.3 us
    all_to_all x1, starting transfers between devices, on_device(): lax.all_to_all(queries[0], 'sp', split_axis=1, concat_axis=0, tiled=True,...  12.4 us
    all_to_all x1, waiting for transfers between devices, on_device(): lax.all_to_all(queries[0], 'sp', split_axis=1, concat_axis=0, tiled=True,...  7.91 us
    ppermute x1, starting transfers between devices, on_device(): key_next = lax.ppermute(key_block, 'blk', behind)  7.88 us
  transfers between devices with their start and end apart: 12, of which 6 were waited for; matrix products, arithmetic and copies ran while one was open for 3% of the time, Pallas kernels for 3%

profile of v3, /device:TPU:74, one launch (start us, length us, event | category | flops | bytes accessed | tf_op | source)
XLA Modules:
  0.0 250.3 jit_solution(7219096815760794147)
XLA Ops:
  6.5 0.0 copy-start.1
  6.6 0.0 all-gather.2.cloned.1.call-start
  6.6 1.1 constant_dynamic-slice_fusion
  7.6 0.7 pad_maximum_fusion
  8.3 0.1 all-gather.2.cloned.1.call-update
  8.4 0.0 copy-start.2
  8.4 1.6 fusion
  10.0 0.0 copy-done.1
  10.0 0.0 copy-done.3
  10.0 0.3 fusion.2
  10.4 0.0 copy-start.4
  10.4 0.0 copy-start.5
  10.4 3.2 %collective-permute-start = (bf16[128,2048]{1,0:T(8,128)(2,1)S(1)}, bf16[128,2048]{1,0:T(8,128)(2,1)S(1)}, u32[]{:S(2)}, u32[]{:S(2)}) collective-permute-start(bf16[128,2048]{1,0:T(8,128)(2,1)S(1)} %constant_dynamic-slice_fusion.2), channel_id=1, source_target_pairs={{0,2},{2,0},{4,6},{6,4},{8,10},{10,8},{12,14},{14,12},{1,3},{3,1},... | collective-permute-start | bytes 1572872 | tf_op jit(solution)/shard_map/ppermute | solution.py:317
  13.7 0.0 copy-done.2
  13.7 0.4 all_to_all.45
  14.1 0.9 copy.10
  15.0 12.4 %all-to-all-start = ((bf16[128,4,512]{2,0,1:T(8,128)(2,1)}), bf16[128,4,512]{2,0,1:T(8,128)(2,1)S(1)}, u32[]{:S(2)}, u32[]{:S(2)}) async-start(bf16[128,4,512]{2,0,1:T(8,128)(2,1)} %copy.10), calls=%async_computation | async-start | bytes 1048576 | tf_op jit(solution)/shard_map/all_to_all | solution.py:329
  27.4 0.0 copy-done.4
  27.4 0.1 dynamic_slice.16
  27.5 0.0 copy-done.5
  27.5 0.1 dynamic_slice.17
  27.6 0.6 maximum_convert_fusion.bias_ref
  28.2 0.0 collective-permute-done
  28.2 1.9 collective-permute-start.1
  30.1 0.5 fusion.3
  30.7 0.8 pad_maximum_fusion.1.cosine_ref
  31.4 0.8 pad_maximum_fusion.2.sine_ref
  32.2 0.0 collective-permute-done.1
  32.2 0.1 broadcast_select_fusion.1
  32.3 1.5 maximum_maximum_fusion.tokens_ref
  33.8 7.9 %all-to-all-done = bf16[128,4,512]{2,0,1:T(8,128)(2,1)S(1)} async-done(((bf16[128,4,512]{2,0,1:T(8,128)(2,1)}), bf16[128,4,512]{2,0,1:T(8,128)(2,1)S(1)}, u32[]{:S(2)}, u32[]{:S(2)}) %all-to-all-start) | async-done | bytes 524320 | tf_op jit(solution)/shard_map/all_to_all | solution.py:329
  41.7 84.0 %all-gather.2.cloned.1.call-done.weight_ref = bf16[4096,512]{1,0:T(8,128)(2,1)} async-done(((bf16[256,512]{1,0:T(8,128)(2,1)}), bf16[4096,512]{1,0:T(8,128)(2,1)}) %all-gather.2.cloned.1.call-update) | async-done | bytes 4194320 | tf_op jit(solution)/shard_map/all_gather | solution.py:310
  125.6 5.3 %project.1 = bf16[256,512]{1,0:T(8,128)(2,1)} custom-call(bf16[256,4096]{1,0:T(8,128)(2,1)} %maximum_maximum_fusion.tokens_ref, bf16[4096,512]{1,0:T(8,128)(2,1)} %all-gather.2.cloned.1.call-done.weight_ref, f32[1,512]{1,0:T(1,128)} %maximum_convert_fusion.bias_ref, f32[256,128]{1,0:T(8,128)} %pad_maximum_fusion.1.cosine_ref, ...), custom_call_target="tpu_custom_call" | custom-call | flops 1073741824 | bytes 6291456 | tf_op jit(solution)/shard_map/project/pallas_call | solution.py:61
  130.9 1.0 fusion.6
  131.9 2.3 collective-permute-start.2
  134.2 0.7 collective-permute-start.3
  134.9 3.9 %collective-permute-done.2 = bf16[128,512]{1,0:T(8,128)(2,1)S(1)} collective-permute-done((bf16[128,512]{1,0:T(8,128)(2,1)S(1)}, bf16[128,512]{1,0:T(8,128)(2,1)S(1)}, u32[]{:S(2)}, u32[]{:S(2)}) %collective-permute-start.2) | collective-permute-done | bytes 131104 | tf_op jit(solution)/shard_map/ppermute | solution.py:346
  138.8 0.0 collective-permute-done.3
  138.8 0.1 copy.13
  139.0 0.9 tile.5
  139.8 6.8 %all-to-all-start.2 = ((bf16[128,16,128]{0,2,1:T(8,128)(2,1)}), bf16[128,16,128]{0,2,1:T(8,128)(2,1)S(1)}, u32[]{:S(2)}, u32[]{:S(2)}) async-start(bf16[128,16,128]{0,2,1:T(8,128)(2,1)} %bitcast.10), calls=%async_computation.2 | async-start | bytes 1048576 | tf_op jit(solution)/shard_map/all_to_all | solution.py:356
  146.6 0.0 copy-start
  146.6 0.1 copy.11
  146.8 20.0 %all-to-all-done.2 = bf16[128,16,128]{0,2,1:T(8,128)(2,1)S(1)} async-done(((bf16[128,16,128]{0,2,1:T(8,128)(2,1)}), bf16[128,16,128]{0,2,1:T(8,128)(2,1)S(1)}, u32[]{:S(2)}, u32[]{:S(2)}) %all-to-all-start.2) | async-done | bytes 524320 | tf_op jit(solution)/shard_map/all_to_all | solution.py:356
  166.8 0.9 tile.4
  167.7 6.5 %all-to-all-start.1 = ((bf16[128,16,128]{0,2,1:T(8,128)(2,1)}), bf16[128,16,128]{0,2,1:T(8,128)(2,1)S(1)}, u32[]{:S(2)}, u32[]{:S(2)}) async-start(bf16[128,16,128]{0,2,1:T(8,128)(2,1)} %bitcast.7), calls=%async_computation.1 | async-start | bytes 1048576 | tf_op jit(solution)/shard_map/all_to_all | solution.py:356
  174.2 0.3 copy.14
  174.5 7.7 %collective-permute-start.6 = (bf16[2048,128]{1,0:T(8,128)(2,1)S(1)}, bf16[2048,128]{1,0:T(8,128)(2,1)S(1)}, u32[]{:S(2)}, u32[]{:S(2)}) collective-permute-start(bf16[2048,128]{1,0:T(8,128)(2,1)S(1)} %bitcast.30), channel_id=1, source_target_pairs={{2,0},{4,2},{6,4},{8,6},{10,8},{12,10},{14,12},{0,14},{3,1},{5,3},... | collective-permute-start | bytes 1572872 | tf_op jit(solution)/shard_map/ppermute | solution.py:364
  182.3 2.0 collective-permute-start.7
  184.2 11.0 %all-to-all-done.1 = bf16[128,16,128]{0,2,1:T(8,128)(2,1)S(1)} async-done(((bf16[128,16,128]{0,2,1:T(8,128)(2,1)}), bf16[128,16,128]{0,2,1:T(8,128)(2,1)S(1)}, u32[]{:S(2)}, u32[]{:S(2)}) %all-to-all-start.1) | async-done | bytes 524320 | tf_op jit(solution)/shard_map/all_to_all | solution.py:356
  195.2 0.3 copy.12
  195.5 7.9 %collective-permute-start.4 = (bf16[2048,128]{1,0:T(8,128)(2,1)S(1)}, bf16[2048,128]{1,0:T(8,128)(2,1)S(1)}, u32[]{:S(2)}, u32[]{:S(2)}) collective-permute-start(bf16[2048,128]{1,0:T(8,128)(2,1)S(1)} %bitcast.33), channel_id=1, source_target_pairs={{2,0},{4,2},{6,4},{8,6},{10,8},{12,10},{14,12},{0,14},{3,1},{5,3},... | collective-permute-start | bytes 1572872 | tf_op jit(solution)/shard_map/ppermute | solution.py:362
  203.4 2.1 collective-permute-start.5
  205.6 0.1 pad_add_fusion.1.info
  205.6 0.1 pad_add_fusion.info
  205.7 0.0 copy-done
  205.7 8.2 %attend_first.1 = (f32[4,512,128]{2,1,0:T(8,128)S(1)}, f32[4,512,256]{2,1,0:T(8,128)S(1)}) custom-call(s32[2]{0:T(128)S(1)} %pad_add_fusion.1.info, s32[8]{0:T(128)S(1)} %copy-done, bf16[512,512]{1,0:T(8,128)(2,1)S(1)} %bitcast.28, bf16[2048,128]{1,0:T(8,128)(2,1)S(1)} %bitcast.35, bf16[2048,128]{1,0:T(8,128)(2,1)S(1)} %bitcast.32), custom_call_target="tpu_custom_call" | custom-call | flops 2147483648 | bytes 4194304 | tf_op jit(solution)/shard_map/attend_first/pallas_call | solution.py:258
  213.9 0.0 collective-permute-done.6.refs_2_
  213.9 0.0 collective-permute-done.7.refs_3_
  213.9 0.0 collective-permute-done.4.refs_0_
  213.9 0.7 collective-permute-done.5.refs_1_
  214.6 13.5 %attend_last.1 = bf16[512,512]{1,0:T(8,128)(2,1)S(1)} custom-call(s32[3]{0:T(128)S(1)} %pad_add_fusion.info, s32[8]{0:T(128)S(1)} %copy-done, bf16[512,512]{1,0:T(8,128)(2,1)S(1)} %bitcast.29, bf16[2048,128]{1,0:T(8,128)(2,1)S(1)} %collective-permute-done.4.refs_0_, bf16[2048,128]{1,0:T(8,128)(2,1)} %collective-permute-done.5.refs_1_, ...), custom_call_target="tpu_custom_call" | custom-call | flops 4294967296 | bytes 4194304 | tf_op jit(solution)/shard_map/attend_last/pallas_call | solution.py:258
  228.2 14.4 %all_to_all.62 = bf16[4,128,512]{2,1,0:T(8,128)(2,1)S(1)} all-to-all(bf16[4,128,512]{2,1,0:T(8,128)(2,1)S(1)} %bitcast.36), channel_id=1, replica_groups={{0,16,32,48},{64,80,96,112},{128,144,160,176},{192,208,224,240},{1,17,3..., dimensions={0} | all-to-all | bytes 1048576 | tf_op jit(solution)/shard_map/all_to_all | solution.py:381
  242.6 0.8 maximum_bitcast_fusion
  (12 shorter events, 0.2 us)
Async XLA Ops:
  6.5 3.5 %copy-start.1 = (bf16[1,128,4096]{2,1,0:T(8,128)(2,1)S(1)}, bf16[1,128,4096]{2,1,0:T(8,128)(2,1)}, u32[]{:S(2)}) copy-start(bf16[1,128,4096]{2,1,0:T(8,128)(2,1)} %param.8) | copy-start | bytes 3145732
  6.5 3.5 %copy-start.3 = (f32[4096]{0:T(1024)S(1)}, f32[4096]{0:T(1024)}, u32[]{:S(2)}) copy-start(f32[4096]{0:T(1024)} %param.10) | copy-start | bytes 49156
  6.6 119.1 %all-gather.2.cloned.1.call-start = ((), (), s32[]{:S(2)}) async-start(), calls=%async_computation.4 | async-start | bytes 4456448 | tf_op jit(solution)/shard_map/all_gather | solution.py:310
  8.4 5.3 %copy-start.2 = (bf16[1,128,2048]{2,1,0:T(8,128)(2,1)S(1)}, bf16[1,128,2048]{2,1,0:T(8,128)(2,1)}, u32[]{:S(2)}) copy-start(bf16[1,128,2048]{2,1,0:T(8,128)(2,1)} %param.9) | copy-start | bytes 1572868
  10.4 17.0 %copy-start.4 = (bf16[512]{0:T(512)(128)(2,1)S(1)}, bf16[512]{0:T(512)(128)(2,1)}, u32[]{:S(2)}) copy-start(bf16[512]{0:T(512)(128)(2,1)} %param.13) | copy-start | bytes 3076
  10.4 17.1 %copy-start.5 = (bf16[512]{0:T(512)(128)(2,1)S(1)}, bf16[512]{0:T(512)(128)(2,1)}, u32[]{:S(2)}) copy-start(bf16[512]{0:T(512)(128)(2,1)} %param.14) | copy-start | bytes 3076
  10.4 17.7 %collective-permute-start = (bf16[128,2048]{1,0:T(8,128)(2,1)S(1)}, bf16[128,2048]{1,0:T(8,128)(2,1)S(1)}, u32[]{:S(2)}, u32[]{:S(2)}) collective-permute-start(bf16[128,2048]{1,0:T(8,128)(2,1)S(1)} %constant_dynamic-slice_fusion.2), channel_id=1, source_target_pairs={{0,2},{2,0},{4,6},{6,4},{8,10},{10,8},{12,14},{14,12},{1,3},{3,1},... | collective-permute-start | bytes 1572872 | tf_op jit(solution)/shard_map/ppermute | solution.py:317
  15.0 26.7 %all-to-all-start = ((bf16[128,4,512]{2,0,1:T(8,128)(2,1)}), bf16[128,4,512]{2,0,1:T(8,128)(2,1)S(1)}, u32[]{:S(2)}, u32[]{:S(2)}) async-start(bf16[128,4,512]{2,0,1:T(8,128)(2,1)} %copy.10), calls=%async_computation | async-start | bytes 1048576 | tf_op jit(solution)/shard_map/all_to_all | solution.py:329
  28.2 4.0 %collective-permute-start.1 = (bf16[128,2048]{1,0:T(8,128)(2,1)S(1)}, bf16[128,2048]{1,0:T(8,128)(2,1)S(1)}, u32[]{:S(2)}, u32[]{:S(2)}) collective-permute-start(bf16[128,2048]{1,0:T(8,128)(2,1)S(1)} %collective-permute-done), channel_id=1, source_target_pairs={{0,1},{1,0},{2,3},{3,2},{4,5},{5,4},{6,7},{7,6},{8,9},{9,8},{10,11... | collective-permute-start | bytes 1572872 | tf_op jit(solution)/shard_map/ppermute | solution.py:318
  131.9 6.9 %collective-permute-start.2 = (bf16[128,512]{1,0:T(8,128)(2,1)S(1)}, bf16[128,512]{1,0:T(8,128)(2,1)S(1)}, u32[]{:S(2)}, u32[]{:S(2)}) collective-permute-start(bf16[128,512]{1,0:T(8,128)(2,1)S(1)} %get-tuple-element.29), channel_id=1, source_target_pairs={{0,2},{2,4},{4,6},{6,8},{8,10},{10,12},{12,14},{14,0},{1,3},{3,5},... | collective-permute-start | bytes 393224 | tf_op jit(solution)/shard_map/ppermute | solution.py:346
  134.2 4.6 %collective-permute-start.3 = (bf16[128,512]{1,0:T(8,128)(2,1)S(1)}, bf16[128,512]{1,0:T(8,128)(2,1)S(1)}, u32[]{:S(2)}, u32[]{:S(2)}) collective-permute-start(bf16[128,512]{1,0:T(8,128)(2,1)S(1)} %get-tuple-element.30), channel_id=1, source_target_pairs={{0,4},{2,2},{4,8},{6,6},{8,12},{10,10},{12,0},{14,14},{1,5},{3,3},... | collective-permute-start | bytes 393224 | tf_op jit(solution)/shard_map/ppermute | solution.py:347
  139.8 27.0 %all-to-all-start.2 = ((bf16[128,16,128]{0,2,1:T(8,128)(2,1)}), bf16[128,16,128]{0,2,1:T(8,128)(2,1)S(1)}, u32[]{:S(2)}, u32[]{:S(2)}) async-start(bf16[128,16,128]{0,2,1:T(8,128)(2,1)} %bitcast.10), calls=%async_computation.2 | async-start | bytes 1048576 | tf_op jit(solution)/shard_map/all_to_all | solution.py:356
  146.6 59.1 %copy-start = (s32[8]{0:T(128)S(1)}, s32[8]{0:T(128)}, u32[]{:S(2)}) copy-start(s32[8]{0:T(128)} %docs.3) | copy-start | bytes 100
  167.7 27.5 %all-to-all-start.1 = ((bf16[128,16,128]{0,2,1:T(8,128)(2,1)}), bf16[128,16,128]{0,2,1:T(8,128)(2,1)S(1)}, u32[]{:S(2)}, u32[]{:S(2)}) async-start(bf16[128,16,128]{0,2,1:T(8,128)(2,1)} %bitcast.7), calls=%async_computation.1 | async-start | bytes 1048576 | tf_op jit(solution)/shard_map/all_to_all | solution.py:356
  174.5 39.4 %collective-permute-start.6 = (bf16[2048,128]{1,0:T(8,128)(2,1)S(1)}, bf16[2048,128]{1,0:T(8,128)(2,1)S(1)}, u32[]{:S(2)}, u32[]{:S(2)}) collective-permute-start(bf16[2048,128]{1,0:T(8,128)(2,1)S(1)} %bitcast.30), channel_id=1, source_target_pairs={{2,0},{4,2},{6,4},{8,6},{10,8},{12,10},{14,12},{0,14},{3,1},{5,3},... | collective-permute-start | bytes 1572872 | tf_op jit(solution)/shard_map/ppermute | solution.py:364
  182.3 31.6 %collective-permute-start.7 = (bf16[2048,128]{1,0:T(8,128)(2,1)S(1)}, bf16[2048,128]{1,0:T(8,128)(2,1)S(1)}, u32[]{:S(2)}, u32[]{:S(2)}) collective-permute-start(bf16[2048,128]{1,0:T(8,128)(2,1)S(1)} %bitcast.31), channel_id=1, source_target_pairs={{0,2},{2,4},{4,6},{6,8},{8,10},{10,12},{12,14},{14,0},{1,3},{3,5},... | collective-permute-start | bytes 1572872 | tf_op jit(solution)/shard_map/ppermute | solution.py:365
  195.5 18.4 %collective-permute-start.4 = (bf16[2048,128]{1,0:T(8,128)(2,1)S(1)}, bf16[2048,128]{1,0:T(8,128)(2,1)S(1)}, u32[]{:S(2)}, u32[]{:S(2)}) collective-permute-start(bf16[2048,128]{1,0:T(8,128)(2,1)S(1)} %bitcast.33), channel_id=1, source_target_pairs={{2,0},{4,2},{6,4},{8,6},{10,8},{12,10},{14,12},{0,14},{3,1},{5,3},... | collective-permute-start | bytes 1572872 | tf_op jit(solution)/shard_map/ppermute | solution.py:362
  203.4 11.2 %collective-permute-start.5 = (bf16[2048,128]{1,0:T(8,128)(2,1)S(1)}, bf16[2048,128]{1,0:T(8,128)(2,1)}, u32[]{:S(2)}, u32[]{:S(2)}) collective-permute-start(bf16[2048,128]{1,0:T(8,128)(2,1)S(1)} %bitcast.34), channel_id=1, source_target_pairs={{0,2},{2,4},{4,6},{6,8},{8,10},{10,12},{12,14},{14,0},{1,3},{3,5},... | collective-permute-start | bytes 1572872 | tf_op jit(solution)/shard_map/ppermute | solution.py:363
Sparse Core Ops, SparseCore 0:
  9.4 116.1 all-gather.1

commit v4 on v3

--- a/solution.py
+++ b/solution.py
@@ -30,54 +30,37 @@
     return jnp.concatenate([cosine, cosine], axis=1), jnp.concatenate([-sine, sine], axis=1)
 
 
-def project_kernel(heads, tokens_ref, weight_ref, bias_ref, cosine_ref, sine_ref, out_ref, total):
-    step = pl.program_id(0)
-    product = jnp.dot(tokens_ref[...], weight_ref[...], preferred_element_type=jnp.float32)
-
-    @pl.when(step == 0)
-    def _():
-        total[...] = product
-
-    @pl.when(step > 0)
-    def _():
-        total[...] += product
-
-    @pl.when(step == pl.num_programs(0) - 1)
-    def _():
-        for h in range(heads):
-            columns = slice(h * HEAD, (h + 1) * HEAD)
-            key = total[:, columns] + bias_ref[:, columns]
-            turned = key * cosine_ref[...] + pltpu.roll(key, HEAD // 2, 1) * sine_ref[...]
-            out_ref[:, columns] = turned.astype(jnp.bfloat16)
-        rest = slice(heads * HEAD, 2 * heads * HEAD)
-        out_ref[:, rest] = (total[:, rest] + bias_ref[:, rest]).astype(jnp.bfloat16)
+def project_kernel(
+    heads, tokens_ref, weight_ref, bias_ref, cosine_ref, sine_ref, own_ref, other_ref
+):
+    total = jnp.dot(tokens_ref[...], weight_ref[...], preferred_element_type=jnp.float32)
+    half = own_ref.shape[0]
+    for h in range(2 * heads):
+        columns = slice(h * HEAD, (h + 1) * HEAD)
+        made = total[:, columns] + bias_ref[:, columns]
+        if h < heads:
+            made = made * cosine_ref[...] + pltpu.roll(made, HEAD // 2, 1) * sine_ref[...]
+        made = made.astype(jnp.bfloat16)
+        own_ref[:, columns] = made[:half]
+        other_ref[:, columns] = made[half:]
 
 
 def project(tokens, weight, bias, cosine, sine):
     rows, width = tokens.shape
     columns = weight.shape[1]
-    depth = 1024
-    whole = lambda shape: pl.BlockSpec(shape, lambda k: (0, 0))
+    vmem = pl.BlockSpec(memory_space=pltpu.VMEM)
     return pl.pallas_call(
         functools.partial(project_kernel, columns // (2 * HEAD)),
-        out_shape=jax.ShapeDtypeStruct((rows, columns), jnp.bfloat16),
-        grid=(width // depth,),
-        in_specs=[
-            pl.BlockSpec((rows, depth), lambda k: (0, k)),
-            pl.BlockSpec((depth, columns), lambda k: (k, 0)),
-            whole((1, columns)),
-            whole((rows, HEAD)),
-            whole((rows, HEAD)),
-        ],
-        out_specs=whole((rows, columns)),
-        scratch_shapes=[pltpu.VMEM((rows, columns), jnp.float32)],
+        out_shape=(jax.ShapeDtypeStruct((rows // 2, columns), jnp.bfloat16),) * 2,
+        in_specs=[vmem] * 5,
+        out_specs=(vmem, vmem),
         name="project",
         cost_estimate=pl.CostEstimate(
             flops=2 * rows * width * columns,
             bytes_accessed=2 * (rows + columns) * width,
             transcendentals=0,
         ),
-        compiler_params=pltpu.CompilerParams(vmem_limit_bytes=58 << 20),
+        compiler_params=pltpu.CompilerParams(vmem_limit_bytes=24 << 20),
     )(tokens, weight, bias, cosine, sine)
 
 
@@ -221,8 +204,8 @@
                 ).astype(jnp.bfloat16)
 
 
-def attend(info, docs, query, keys, values, state, last, part=0, parts=1):
-    tokens = query.shape[0] // parts
+def attend(info, docs, query, keys, values, state, last):
+    tokens = query.shape[0]
     heads = query.shape[1] // HEAD
     tiles = tokens // TILE
     blocks = len(keys)
@@ -247,19 +230,11 @@
         )
         out_specs = (vmem, vmem)
     operands = [query, *keys, *values] + ([] if first else list(state))
-    specs = [pl.BlockSpec((tokens, heads * HEAD), lambda _: (part, 0), memory_space=pltpu.VMEM)]
-    specs += [vmem] * (2 * blocks)
-    if not first:
-        specs += [
-            pl.BlockSpec(shape, lambda _: (part, 0, 0), memory_space=pltpu.VMEM)
-            for shape in (max_shape, sum_shape)
-        ]
     pairs = tokens * heads * keys[0].shape[0] * blocks
     return pl.pallas_call(
         functools.partial(attention_kernel, blocks, heads, first, last),
         out_shape=out_shape,
-        grid=(1,),
-        in_specs=[smem, smem] + specs,
+        in_specs=[smem, smem] + [vmem] * len(operands),
         out_specs=out_specs,
         scratch_shapes=scratch,
         name="attend_last" if last else "attend_first",
@@ -342,10 +317,10 @@
     )
     cosine, sine = rotation(places.astype(jnp.float32))
     both, query, bias, cosine, sine = lax.optimization_barrier((both, query, bias, cosine, sine))
-    made = project(both, weight, bias, cosine, sine)
-    near_half = lax.ppermute(made[:local_rows], "blk", ahead)
+    own_made, other_made = project(both, weight, bias, cosine, sine)
+    near_half = lax.ppermute(own_made, "blk", ahead)
     far_half = lax.ppermute(
-        made[local_rows:], "blk", [(b, ((b ^ 1) + 1) % blk_count) for b in range(blk_count)]
+        other_made, "blk", [(b, ((b ^ 1) + 1) % blk_count) for b in range(blk_count)]
     )
     odd = side == 1
 

time: 251 us -> 250 us (level)
  the two profiles are of different devices: /device:TPU:74 before, /device:TPU:68 now
where the time goes in v4:
time: 250 us
  waiting for transfers between devices  133 us (53%)
  starting transfers between devices  51.5 us (21%)
  Pallas kernels  23.1 us (9%)
  blocking collectives  14.4 us (6%)
  between operations  13.8 us (6%)
  local copies, waits for them, and re-layouts  8.35 us (3%)
  other arithmetic  5.92 us (2%)
    all_gather x1, waiting for transfers between devices, on_device(): weight = lax.all_gather(picked, 'sp', axis=0, tiled=True)  83.9 us
    all_to_all x2, waiting for transfers between devices, to_heads(): lax.all_to_all(jnp.tile(heads, (1, quads)), 'sp', split_axis=1, concat_ax...  37 us
    pallas_call x2, Pallas kernels, attend(): pl.pallas_call(functools.partial(attention_kernel, blocks, heads, first,...  21.7 us
    all_to_all x1, blocking collectives, on_device(): lax.all_to_all(result.reshape(kv_local, local_rows, result.shape[1]), 'sp...  14.4 us
    all_to_all x2, starting transfers between devices, to_heads(): lax.all_to_all(jnp.tile(heads, (1, quads)), 'sp', split_axis=1, concat_ax...  13.4 us
    all_to_all x1, starting transfers between devices, on_device(): lax.all_to_all(queries[0], 'sp', split_axis=1, concat_axis=0, tiled=True,...  12.4 us
    all_to_all x1, waiting for transfers between devices, on_device(): lax.all_to_all(queries[0], 'sp', split_axis=1, concat_axis=0, tiled=True,...  8.75 us
    ppermute x1, starting transfers between devices, on_device(): lax.ppermute(other_made, 'blk', [(b, ((b ^ 1) + 1) % blk_count) for b in...  5.58 us
  transfers between devices with their start and end apart: 12, of which 6 were waited for; matrix products, arithmetic and copies ran while one was open for 2% of the time, Pallas kernels for 3%

profile of v4, /device:TPU:68, one launch (start us, length us, event | category | flops | bytes accessed | tf_op | source)
XLA Modules:
  0.0 250.3 jit_solution(15730139671798787036)
XLA Ops:
  6.5 0.0 copy-start.3
  6.5 0.0 copy-start.5
  6.6 0.0 all-gather.2.cloned.1.call-start
  6.6 1.1 constant_dynamic-slice_fusion
  7.6 0.7 pad_maximum_fusion
  8.4 0.1 all-gather.2.cloned.1.call-update
  8.4 0.0 copy-start.4
  8.4 1.6 fusion
  10.0 0.0 copy-done.3
  10.0 0.0 copy-done.5
  10.0 0.3 fusion.2
  10.4 0.0 copy-start.2
  10.4 1.0 copy-done.2
  11.4 3.6 %collective-permute-start = (bf16[128,2048]{1,0:T(8,128)(2,1)S(1)}, bf16[128,2048]{1,0:T(8,128)(2,1)S(1)}, u32[]{:S(2)}, u32[]{:S(2)}) collective-permute-start(bf16[128,2048]{1,0:T(8,128)(2,1)S(1)} %constant_dynamic-slice_fusion.2), channel_id=1, source_target_pairs={{0,2},{2,0},{4,6},{6,4},{8,10},{10,8},{12,14},{14,12},{1,3},{3,1},... | collective-permute-start | bytes 1572872 | tf_op jit(solution)/shard_map/ppermute | solution.py:292
  15.0 0.0 copy-done.4
  15.0 0.4 all_to_all.45
  15.4 0.9 copy.10
  16.3 12.4 %all-to-all-start = ((bf16[128,4,512]{2,0,1:T(8,128)(2,1)}), bf16[128,4,512]{2,0,1:T(8,128)(2,1)S(1)}, u32[]{:S(2)}, u32[]{:S(2)}) async-start(bf16[128,4,512]{2,0,1:T(8,128)(2,1)} %copy.10), calls=%async_computation | async-start | bytes 1048576 | tf_op jit(solution)/shard_map/all_to_all | solution.py:304
  28.7 0.0 copy-done.6
  28.7 0.1 dynamic_slice.16
  28.8 0.0 copy-done.7
  28.8 0.1 dynamic_slice.17
  28.9 0.0 collective-permute-done
  28.9 2.0 collective-permute-start.1
  30.9 0.5 fusion.3
  31.4 0.1 pad_maximum_fusion.1.cosine_ref
  31.5 0.1 pad_maximum_fusion.2.sine_ref
  31.6 1.1 collective-permute-done.1
  32.7 0.1 broadcast_select_fusion.1
  32.8 1.4 maximum_maximum_fusion.tokens_ref
  34.2 8.7 %all-to-all-done = bf16[128,4,512]{2,0,1:T(8,128)(2,1)S(1)} async-done(((bf16[128,4,512]{2,0,1:T(8,128)(2,1)}), bf16[128,4,512]{2,0,1:T(8,128)(2,1)S(1)}, u32[]{:S(2)}, u32[]{:S(2)}) %all-to-all-start) | async-done | bytes 524320 | tf_op jit(solution)/shard_map/all_to_all | solution.py:304
  43.0 83.9 %all-gather.2.cloned.1.call-done.weight_ref = bf16[4096,512]{1,0:T(8,128)(2,1)} async-done(((bf16[256,512]{1,0:T(8,128)(2,1)}), bf16[4096,512]{1,0:T(8,128)(2,1)}) %all-gather.2.cloned.1.call-update) | async-done | bytes 4194320 | tf_op jit(solution)/shard_map/all_gather | solution.py:285
  126.9 2.2 copy-done
  129.1 1.4 project.1
  130.5 2.6 %collective-permute-start.2 = (bf16[128,512]{1,0:T(8,128)(2,1)S(1)}, bf16[128,512]{1,0:T(8,128)(2,1)S(1)}, u32[]{:S(2)}, u32[]{:S(2)}) collective-permute-start(bf16[128,512]{1,0:T(8,128)(2,1)S(1)} %get-tuple-element.19), channel_id=1, source_target_pairs={{0,2},{2,4},{4,6},{6,8},{8,10},{10,12},{12,14},{14,0},{1,3},{3,5},... | collective-permute-start | bytes 393224 | tf_op jit(solution)/shard_map/ppermute | solution.py:321
  133.0 5.6 %collective-permute-start.3 = (bf16[128,512]{1,0:T(8,128)(2,1)S(1)}, bf16[128,512]{1,0:T(8,128)(2,1)S(1)}, u32[]{:S(2)}, u32[]{:S(2)}) collective-permute-start(bf16[128,512]{1,0:T(8,128)(2,1)S(1)} %get-tuple-element.20), channel_id=1, source_target_pairs={{0,4},{2,2},{4,8},{6,6},{8,12},{10,10},{12,0},{14,14},{1,5},{3,3},... | collective-permute-start | bytes 393224 | tf_op jit(solution)/shard_map/ppermute | solution.py:322
  138.6 0.0 collective-permute-done.2
  138.7 2.5 collective-permute-done.3
  141.2 0.1 copy.13
  141.3 0.9 tile.5
  142.2 6.8 %all-to-all-start.2 = ((bf16[128,16,128]{0,2,1:T(8,128)(2,1)}), bf16[128,16,128]{0,2,1:T(8,128)(2,1)S(1)}, u32[]{:S(2)}, u32[]{:S(2)}) async-start(bf16[128,16,128]{0,2,1:T(8,128)(2,1)} %bitcast.10), calls=%async_computation.2 | async-start | bytes 1048576 | tf_op jit(solution)/shard_map/all_to_all | solution.py:331
  149.0 0.0 copy-start.1
  149.0 0.1 copy.11
  149.1 20.0 %all-to-all-done.2 = bf16[128,16,128]{0,2,1:T(8,128)(2,1)S(1)} async-done(((bf16[128,16,128]{0,2,1:T(8,128)(2,1)}), bf16[128,16,128]{0,2,1:T(8,128)(2,1)S(1)}, u32[]{:S(2)}, u32[]{:S(2)}) %all-to-all-start.2) | async-done | bytes 524320 | tf_op jit(solution)/shard_map/all_to_all | solution.py:331
  169.1 0.9 tile.4
  170.0 6.6 %all-to-all-start.1 = ((bf16[128,16,128]{0,2,1:T(8,128)(2,1)}), bf16[128,16,128]{0,2,1:T(8,128)(2,1)S(1)}, u32[]{:S(2)}, u32[]{:S(2)}) async-start(bf16[128,16,128]{0,2,1:T(8,128)(2,1)} %bitcast.7), calls=%async_computation.1 | async-start | bytes 1048576 | tf_op jit(solution)/shard_map/all_to_all | solution.py:331
  176.6 0.3 copy.14
  177.0 2.0 collective-permute-start.6
  178.9 4.0 %collective-permute-start.7 = (bf16[2048,128]{1,0:T(8,128)(2,1)S(1)}, bf16[2048,128]{1,0:T(8,128)(2,1)S(1)}, u32[]{:S(2)}, u32[]{:S(2)}) collective-permute-start(bf16[2048,128]{1,0:T(8,128)(2,1)S(1)} %bitcast.31), channel_id=1, source_target_pairs={{0,2},{2,4},{4,6},{6,8},{8,10},{10,12},{12,14},{14,0},{1,3},{3,5},... | collective-permute-start | bytes 1572872 | tf_op jit(solution)/shard_map/ppermute | solution.py:340
  182.9 16.9 %all-to-all-done.1 = bf16[128,16,128]{0,2,1:T(8,128)(2,1)S(1)} async-done(((bf16[128,16,128]{0,2,1:T(8,128)(2,1)}), bf16[128,16,128]{0,2,1:T(8,128)(2,1)S(1)}, u32[]{:S(2)}, u32[]{:S(2)}) %all-to-all-start.1) | async-done | bytes 524320 | tf_op jit(solution)/shard_map/all_to_all | solution.py:331
  199.8 0.3 copy.12
  200.1 2.0 collective-permute-start.4
  202.1 4.1 %collective-permute-start.5 = (bf16[2048,128]{1,0:T(8,128)(2,1)S(1)}, bf16[2048,128]{1,0:T(8,128)(2,1)}, u32[]{:S(2)}, u32[]{:S(2)}) collective-permute-start(bf16[2048,128]{1,0:T(8,128)(2,1)S(1)} %bitcast.34), channel_id=1, source_target_pairs={{0,2},{2,4},{4,6},{6,8},{8,10},{10,12},{12,14},{14,0},{1,3},{3,5},... | collective-permute-start | bytes 1572872 | tf_op jit(solution)/shard_map/ppermute | solution.py:338
  206.2 0.1 pad_add_fusion.1.info
  206.3 0.1 pad_add_fusion.info
  206.4 0.0 copy-done.1
  206.4 8.2 %attend_first.1 = (f32[4,512,128]{2,1,0:T(8,128)S(1)}, f32[4,512,256]{2,1,0:T(8,128)S(1)}) custom-call(s32[2]{0:T(128)S(1)} %pad_add_fusion.1.info, s32[8]{0:T(128)S(1)} %copy-done.1, bf16[512,512]{1,0:T(8,128)(2,1)S(1)} %bitcast.28, bf16[2048,128]{1,0:T(8,128)(2,1)S(1)} %bitcast.35, bf16[2048,128]{1,0:T(8,128)(2,1)S(1)} %bitcast.32), custom_call_target="tpu_custom_call" | custom-call | flops 2147483648 | bytes 4194304 | tf_op jit(solution)/shard_map/attend_first/pallas_call | solution.py:234
  214.6 0.0 collective-permute-done.6.refs_2_
  214.6 0.0 collective-permute-done.7.refs_3_
  214.6 0.0 collective-permute-done.4.refs_0_
  214.6 0.0 collective-permute-done.5.refs_1_
  214.6 13.6 %attend_last.1 = bf16[512,512]{1,0:T(8,128)(2,1)S(1)} custom-call(s32[3]{0:T(128)S(1)} %pad_add_fusion.info, s32[8]{0:T(128)S(1)} %copy-done.1, bf16[512,512]{1,0:T(8,128)(2,1)S(1)} %bitcast.29, bf16[2048,128]{1,0:T(8,128)(2,1)S(1)} %collective-permute-done.4.refs_0_, bf16[2048,128]{1,0:T(8,128)(2,1)} %collective-permute-done.5.refs_1_, ...), custom_call_target="tpu_custom_call" | custom-call | flops 4294967296 | bytes 4194304 | tf_op jit(solution)/shard_map/attend_last/pallas_call | solution.py:234
  228.2 14.4 %all_to_all.62 = bf16[4,128,512]{2,1,0:T(8,128)(2,1)S(1)} all-to-all(bf16[4,128,512]{2,1,0:T(8,128)(2,1)S(1)} %bitcast.36), channel_id=1, replica_groups={{0,16,32,48},{64,80,96,112},{128,144,160,176},{192,208,224,240},{1,17,3..., dimensions={0} | all-to-all | bytes 1048576 | tf_op jit(solution)/shard_map/all_to_all | solution.py:356
  242.6 0.8 maximum_bitcast_fusion
  (15 shorter events, 0.2 us)
Async XLA Ops:
  6.5 3.5 %copy-start.3 = (bf16[1,128,4096]{2,1,0:T(8,128)(2,1)S(1)}, bf16[1,128,4096]{2,1,0:T(8,128)(2,1)}, u32[]{:S(2)}) copy-start(bf16[1,128,4096]{2,1,0:T(8,128)(2,1)} %param.8) | copy-start | bytes 3145732
  6.5 3.5 %copy-start.5 = (f32[4096]{0:T(1024)S(1)}, f32[4096]{0:T(1024)}, u32[]{:S(2)}) copy-start(f32[4096]{0:T(1024)} %param.10) | copy-start | bytes 49156
  6.6 120.3 %all-gather.2.cloned.1.call-start = ((), (), s32[]{:S(2)}) async-start(), calls=%async_computation.4 | async-start | bytes 4456448 | tf_op jit(solution)/shard_map/all_gather | solution.py:285
  8.4 6.6 %copy-start.4 = (bf16[1,128,2048]{2,1,0:T(8,128)(2,1)S(1)}, bf16[1,128,2048]{2,1,0:T(8,128)(2,1)}, u32[]{:S(2)}) copy-start(bf16[1,128,2048]{2,1,0:T(8,128)(2,1)} %param.9) | copy-start | bytes 1572868
  10.4 1.0 copy-start.2
  11.4 17.3 %copy-start.6 = (bf16[512]{0:T(512)(128)(2,1)S(1)}, bf16[512]{0:T(512)(128)(2,1)}, u32[]{:S(2)}) copy-start(bf16[512]{0:T(512)(128)(2,1)} %param.13) | copy-start | bytes 3076
  11.4 17.4 %copy-start.7 = (bf16[512]{0:T(512)(128)(2,1)S(1)}, bf16[512]{0:T(512)(128)(2,1)}, u32[]{:S(2)}) copy-start(bf16[512]{0:T(512)(128)(2,1)} %param.14) | copy-start | bytes 3076
  11.4 17.5 %collective-permute-start = (bf16[128,2048]{1,0:T(8,128)(2,1)S(1)}, bf16[128,2048]{1,0:T(8,128)(2,1)S(1)}, u32[]{:S(2)}, u32[]{:S(2)}) collective-permute-start(bf16[128,2048]{1,0:T(8,128)(2,1)S(1)} %constant_dynamic-slice_fusion.2), channel_id=1, source_target_pairs={{0,2},{2,0},{4,6},{6,4},{8,10},{10,8},{12,14},{14,12},{1,3},{3,1},... | collective-permute-start | bytes 1572872 | tf_op jit(solution)/shard_map/ppermute | solution.py:292
  16.3 26.7 %all-to-all-start = ((bf16[128,4,512]{2,0,1:T(8,128)(2,1)}), bf16[128,4,512]{2,0,1:T(8,128)(2,1)S(1)}, u32[]{:S(2)}, u32[]{:S(2)}) async-start(bf16[128,4,512]{2,0,1:T(8,128)(2,1)} %copy.10), calls=%async_computation | async-start | bytes 1048576 | tf_op jit(solution)/shard_map/all_to_all | solution.py:304
  28.9 3.8 %collective-permute-start.1 = (bf16[128,2048]{1,0:T(8,128)(2,1)S(1)}, bf16[128,2048]{1,0:T(8,128)(2,1)S(1)}, u32[]{:S(2)}, u32[]{:S(2)}) collective-permute-start(bf16[128,2048]{1,0:T(8,128)(2,1)S(1)} %collective-permute-done), channel_id=1, source_target_pairs={{0,1},{1,0},{2,3},{3,2},{4,5},{5,4},{6,7},{7,6},{8,9},{9,8},{10,11... | collective-permute-start | bytes 1572872 | tf_op jit(solution)/shard_map/ppermute | solution.py:293
  126.9 2.2 copy-start
  130.5 8.2 %collective-permute-start.2 = (bf16[128,512]{1,0:T(8,128)(2,1)S(1)}, bf16[128,512]{1,0:T(8,128)(2,1)S(1)}, u32[]{:S(2)}, u32[]{:S(2)}) collective-permute-start(bf16[128,512]{1,0:T(8,128)(2,1)S(1)} %get-tuple-element.19), channel_id=1, source_target_pairs={{0,2},{2,4},{4,6},{6,8},{8,10},{10,12},{12,14},{14,0},{1,3},{3,5},... | collective-permute-start | bytes 393224 | tf_op jit(solution)/shard_map/ppermute | solution.py:321
  133.0 8.1 %collective-permute-start.3 = (bf16[128,512]{1,0:T(8,128)(2,1)S(1)}, bf16[128,512]{1,0:T(8,128)(2,1)S(1)}, u32[]{:S(2)}, u32[]{:S(2)}) collective-permute-start(bf16[128,512]{1,0:T(8,128)(2,1)S(1)} %get-tuple-element.20), channel_id=1, source_target_pairs={{0,4},{2,2},{4,8},{6,6},{8,12},{10,10},{12,0},{14,14},{1,5},{3,3},... | collective-permute-start | bytes 393224 | tf_op jit(solution)/shard_map/ppermute | solution.py:322
  142.2 27.0 %all-to-all-start.2 = ((bf16[128,16,128]{0,2,1:T(8,128)(2,1)}), bf16[128,16,128]{0,2,1:T(8,128)(2,1)S(1)}, u32[]{:S(2)}, u32[]{:S(2)}) async-start(bf16[128,16,128]{0,2,1:T(8,128)(2,1)} %bitcast.10), calls=%async_computation.2 | async-start | bytes 1048576 | tf_op jit(solution)/shard_map/all_to_all | solution.py:331
  149.0 57.4 %copy-start.1 = (s32[8]{0:T(128)S(1)}, s32[8]{0:T(128)}, u32[]{:S(2)}) copy-start(s32[8]{0:T(128)} %docs.3) | copy-start | bytes 100
  170.0 29.8 %all-to-all-start.1 = ((bf16[128,16,128]{0,2,1:T(8,128)(2,1)}), bf16[128,16,128]{0,2,1:T(8,128)(2,1)S(1)}, u32[]{:S(2)}, u32[]{:S(2)}) async-start(bf16[128,16,128]{0,2,1:T(8,128)(2,1)} %bitcast.7), calls=%async_computation.1 | async-start | bytes 1048576 | tf_op jit(solution)/shard_map/all_to_all | solution.py:331
  177.0 37.6 %collective-permute-start.6 = (bf16[2048,128]{1,0:T(8,128)(2,1)S(1)}, bf16[2048,128]{1,0:T(8,128)(2,1)S(1)}, u32[]{:S(2)}, u32[]{:S(2)}) collective-permute-start(bf16[2048,128]{1,0:T(8,128)(2,1)S(1)} %bitcast.30), channel_id=1, source_target_pairs={{2,0},{4,2},{6,4},{8,6},{10,8},{12,10},{14,12},{0,14},{3,1},{5,3},... | collective-permute-start | bytes 1572872 | tf_op jit(solution)/shard_map/ppermute | solution.py:339
  178.9 35.7 %collective-permute-start.7 = (bf16[2048,128]{1,0:T(8,128)(2,1)S(1)}, bf16[2048,128]{1,0:T(8,128)(2,1)S(1)}, u32[]{:S(2)}, u32[]{:S(2)}) collective-permute-start(bf16[2048,128]{1,0:T(8,128)(2,1)S(1)} %bitcast.31), channel_id=1, source_target_pairs={{0,2},{2,4},{4,6},{6,8},{8,10},{10,12},{12,14},{14,0},{1,3},{3,5},... | collective-permute-start | bytes 1572872 | tf_op jit(solution)/shard_map/ppermute | solution.py:340
  200.1 14.5 %collective-permute-start.4 = (bf16[2048,128]{1,0:T(8,128)(2,1)S(1)}, bf16[2048,128]{1,0:T(8,128)(2,1)S(1)}, u32[]{:S(2)}, u32[]{:S(2)}) collective-permute-start(bf16[2048,128]{1,0:T(8,128)(2,1)S(1)} %bitcast.33), channel_id=1, source_target_pairs={{2,0},{4,2},{6,4},{8,6},{10,8},{12,10},{14,12},{0,14},{3,1},{5,3},... | collective-permute-start | bytes 1572872 | tf_op jit(solution)/shard_map/ppermute | solution.py:337
  202.1 12.5 %collective-permute-start.5 = (bf16[2048,128]{1,0:T(8,128)(2,1)S(1)}, bf16[2048,128]{1,0:T(8,128)(2,1)}, u32[]{:S(2)}, u32[]{:S(2)}) collective-permute-start(bf16[2048,128]{1,0:T(8,128)(2,1)S(1)} %bitcast.34), channel_id=1, source_target_pairs={{0,2},{2,4},{4,6},{6,8},{8,10},{10,12},{12,14},{14,0},{1,3},{3,5},... | collective-permute-start | bytes 1572872 | tf_op jit(solution)/shard_map/ppermute | solution.py:338
Sparse Core Ops, SparseCore 0:
  9.4 117.4 all-gather.1
